TPU v7x, 256 devices: a whole 4x4x8 slice. The times are simulated.
256 devices in a mesh: section: 8 (over x_hi, y), shard: 32 (over z, x_lo, core).
Axes of the slice: x: 4 (x_hi: 2, x_lo: 2; x = x_hi * 2 + x_lo), y: 4, z: 8, core: 2. Of those that a mesh axis runs over, the one named last changes fastest.
Arguments:
- activations: bfloat16 [8, 3072, 4096], P('section', 'shard'), may hold values from -30 to 30, as said below
- top_grad: bfloat16 [3072, 4096], P('shard'), may hold values from -6 to 6
- loss_mask: int32 [3072], P('shard'), may hold values 0 or 1
- norm_gain: float32 [8, 4096], P('section'), may hold values from 0.5 to 1.5
- value_weight: bfloat16 [8, 4096, 1024], P('section', 'shard'), may hold values from -0.046875 to 0.046875
- output_weight: bfloat16 [8, 1024, 4096], P('section', None, 'shard'), may hold values from -0.09375 to 0.09375
- value_proj: bfloat16 [8, 1024, 64], P('section'), may hold values from -0.1875 to 0.1875
- grad_proj: bfloat16 [8, 4096, 64], P('section'), may hold values from -0.09375 to 0.09375
- store: float32 [8, 4096, 4096], P('section', 'shard'), may hold values from -0.024 to 0.024
Outputs:
- scores: float32 [32, 4096], P('section', 'shard')
Inputs may be any that keep to these rules, and one draw needn't show every extreme that they name: activations of order one per token.
All inputs are finite; a program needn't handle non-finite values. No bound on the sum of `loss_mask` on one device may be relied on, other than what follows from the above.
Results may differ from a plain program's by a relative error of at most 0.007.
Values may be sent and summed in bfloat16 or wider, within the bound.
A program may use at most 128 MiB of HBM per device.

v0:
```python
import jax
import jax.numpy as jnp
from jax import lax
from jax.experimental import pallas as pl
from jax.experimental.pallas import tpu as pltpu
from jax.sharding import PartitionSpec as P

LEN = 96
EPSILON = 1e-05
MESH = pl.DeviceIdType.MESH
NZ = 8
SECTIONS = 8
ROWS = 16
BLOCKS = LEN // ROWS


def chain_kernel(
    act, top, mask, gain, vt_own, ot_own, vproj, gproj,
    feat,
    wvt, wot, normed, rms, c_in, c_out, scaled, va, vlow,
    zs, zr, xs, xr, ds_, dr, cs, cr,
):
    sec = lax.axis_index("section")
    shard = lax.axis_index("shard")
    z = shard // 4
    xl = (shard // 2) % 2
    core = shard % 2
    width = act.shape[1]
    kv = wot.shape[1]
    cols = vt_own.shape[1]

    def dev(z_, x_, c_):
        return (sec, z_ * 4 + x_ * 2 + c_)

    z_next = (z + 1) % NZ
    z_prev = (z + NZ - 1) % NZ
    up = (sec + 1) % SECTIONS
    down = (sec + SECTIONS - 1) % SECTIONS
    barrier = pltpu.get_barrier_semaphore()
    peers = (
        dev(z_next, xl, core), dev(z_prev, xl, core), dev(z, 1 - xl, core), dev(z, xl, 1 - core),
        (up, shard), (down, shard),
    )
    for peer in peers:
        pl.semaphore_signal(barrier, inc=1, device_id=peer, device_id_type=MESH)
    pl.semaphore_wait(barrier, len(peers))

    def v_block(z_, x_, c_, half):
        first = pl.multiple_of((z_ * 4 + x_ * 2 + c_) * cols, cols)
        if half is None:
            return wvt.at[:, pl.ds(first, cols)]
        return wvt.at[pl.ds(half * (kv // 2), kv // 2), pl.ds(first, cols)]

    def o_block(z_, x_, c_, half):
        first = (z_ * 4 + x_ * 2 + c_) * cols
        if half is None:
            return wot.at[pl.ds(pl.multiple_of(first, cols), cols), :]
        return wot.at[pl.ds(pl.multiple_of(first + half * (cols // 2), cols // 2), cols // 2), :]

    def block(item, z_, c_, half):
        if item == 0:
            return v_block(z_, xl, c_, half)
        return o_block(z_, xl if item == 1 else 1 - xl, c_, half)

    def origin(direction, hops):
        return (z + (NZ - hops if direction == 0 else hops)) % NZ

    def z_copy(direction, k, item):
        half = None if k < 3 else direction
        zo = origin(direction, k)
        dst = block(item, zo, core, half)
        src = (vt_own if item == 0 else ot_own) if k == 0 and item < 2 else dst
        return pltpu.make_async_remote_copy(
            src_ref=src, dst_ref=dst, send_sem=zs.at[direction, k, item], recv_sem=zr.at[direction, k, item],
            device_id=dev(z_next if direction == 0 else z_prev, xl, core), device_id_type=MESH,
        )

    def z_arrival(direction, k, item):
        half = None if k < 3 else direction
        ref = block(item, origin(direction, k + 1), core, half)
        return pltpu.make_async_remote_copy(
            src_ref=ref, dst_ref=ref, send_sem=zs.at[direction, k, item], recv_sem=zr.at[direction, k, item],
            device_id=dev(z_prev if direction == 0 else z_next, xl, core), device_id_type=MESH,
        )

    def x_refs(index, x_):
        if index == 0:
            return o_block(z, x_, core, None)
        if index == 1:
            return v_block(z, x_, core, None)
        direction, k = (index - 2) // 4, (index - 2) % 4
        return v_block(origin(direction, k + 1), x_, core, None if k < 3 else direction)

    def x_copy(index):
        dst = x_refs(index, xl)
        src = (ot_own, vt_own)[index] if index < 2 else dst
        return pltpu.make_async_remote_copy(
            src_ref=src, dst_ref=dst, send_sem=xs.at[index], recv_sem=xr.at[index],
            device_id=dev(z, 1 - xl, core), device_id_type=MESH,
        )

    def x_arrival(index):
        ref = x_refs(index, 1 - xl)
        return pltpu.make_async_remote_copy(
            src_ref=ref, dst_ref=ref, send_sem=xs.at[index], recv_sem=xr.at[index],
            device_id=dev(z, 1 - xl, core), device_id_type=MESH,
        )

    def d_refs(index, c_):
        if index == 0:
            return o_block(z, xl, c_, None)
        if index == 1:
            return v_block(z, xl, c_, None)
        if index < 26:
            direction, k, item = (index - 2) // 12, (index - 2) // 3 % 4, (index - 2) % 3
            return block(item, origin(direction, k + 1), c_, None if k < 3 else direction)
        index -= 26
        if index == 0:
            return o_block(z, 1 - xl, c_, None)
        if index == 1:
            return v_block(z, 1 - xl, c_, None)
        direction, k = (index - 2) // 4, (index - 2) % 4
        return v_block(origin(direction, k + 1), 1 - xl, c_, None if k < 3 else direction)

    def d_copy(index):
        dst = d_refs(index, core)
        src = (ot_own, vt_own)[index] if index < 2 else dst
        return pltpu.make_async_remote_copy(
            src_ref=src, dst_ref=dst, send_sem=ds_.at[index], recv_sem=dr.at[index],
            device_id=dev(z, xl, 1 - core), device_id_type=MESH,
        )

    def d_arrival(index):
        ref = d_refs(index, 1 - core)
        return pltpu.make_async_remote_copy(
            src_ref=ref, dst_ref=ref, send_sem=ds_.at[index], recv_sem=dr.at[index],
            device_id=dev(z, xl, 1 - core), device_id_type=MESH,
        )

    started = []

    def start(copy):
        copy.start()
        started.append(copy)

    start(x_copy(0))
    start(x_copy(1))
    for item in (0, 1):
        for direction in (0, 1):
            start(z_copy(direction, 0, item))
    start(d_copy(0))
    start(d_copy(1))
    own = pl.ds(pl.multiple_of(shard * cols, cols), cols)
    wvt[:, own] = vt_own[...]
    wot[own, :] = ot_own[...]

    def prepare(b, carry):
        rows = pl.ds(pl.multiple_of(b * ROWS, ROWS), ROWS)
        hidden = act[rows, :].astype(jnp.float32)
        inverse = lax.rsqrt(jnp.mean(hidden * hidden, axis=-1, keepdims=True) + EPSILON)
        rms[rows, :] = jnp.broadcast_to(inverse, (ROWS, 128))
        normed[rows, :] = (hidden * inverse * gain[...]).astype(jnp.bfloat16)
        return carry

    lax.fori_loop(0, BLOCKS, prepare, 0)

    @pl.when(sec == SECTIONS - 1)
    def _():
        def masked(b, carry):
            rows = pl.ds(pl.multiple_of(b * ROWS, ROWS), ROWS)
            row_at = lax.broadcasted_iota(jnp.int32, (ROWS, LEN), 0) + b * ROWS
            col_at = lax.broadcasted_iota(jnp.int32, (ROWS, LEN), 1)
            kept = jnp.where(row_at == col_at, mask[...].astype(jnp.float32), 0.0)
            column = jnp.sum(kept, axis=-1, keepdims=True)
            c_in[b] = (top[rows, :].astype(jnp.float32) * column).astype(jnp.bfloat16)
            return carry

        lax.fori_loop(0, BLOCKS, masked, 0)

    x_arrival(0).wait_recv()
    for direction in (0, 1):
        start(z_copy(direction, 0, 2))
    start(d_copy(26))
    x_arrival(1).wait_recv()
    start(d_copy(27))
    for k in range(4):
        for item in range(3):
            for direction in (0, 1):
                z_arrival(direction, k, item).wait_recv()
                if k < 3:
                    start(z_copy(direction, k + 1, item))
                if item == 0:
                    start(x_copy(2 + direction * 4 + k))
                start(d_copy(2 + direction * 12 + k * 3 + item))
        for direction in (0, 1):
            x_arrival(2 + direction * 4 + k).wait_recv()
            start(d_copy(26 + 2 + direction * 4 + k))
    for index in range(36):
        d_arrival(index).wait_recv()

    def value_path():
        for n in range(0, kv, 256):
            part = lax.dot_general(
                normed[...], wvt[n : n + 256, :], (((1,), (1,)), ((), ())), preferred_element_type=jnp.float32
            )
            va[:, n : n + 256] = part.astype(jnp.bfloat16)
        vlow[...] = jnp.dot(va[...], vproj[...], preferred_element_type=jnp.float32)

    def c_copy(b):
        return pltpu.make_async_remote_copy(
            src_ref=c_out.at[b], dst_ref=c_in.at[b], send_sem=cs.at[b], recv_sem=cr.at[b],
            device_id=(down, shard), device_id_type=MESH,
        )

    def c_arrival(b):
        return pltpu.make_async_remote_copy(
            src_ref=c_in.at[b], dst_ref=c_in.at[b], send_sem=cs.at[b], recv_sem=cr.at[b],
            device_id=(up, shard), device_id_type=MESH,
        )

    @pl.when(sec < SECTIONS - 1)
    def _():
        value_path()

    def stage(b, carry):
        @pl.when(sec < SECTIONS - 1)
        def _():
            c_arrival(b).wait_recv()

        @pl.when(sec > 0)
        def _():
            rows = pl.ds(pl.multiple_of(b * ROWS, ROWS), ROWS)
            grad_value = jnp.dot(c_in[b], wot[...], preferred_element_type=jnp.float32).astype(jnp.bfloat16)
            total = jnp.zeros((ROWS, 1), jnp.float32)
            step = 512
            for n in range(0, width, step):
                part = jnp.dot(grad_value, wvt[:, n : n + step], preferred_element_type=jnp.float32)
                part = gain[:, n : n + step] * part
                scaled[:, n : n + step] = part
                hidden = act[rows, n : n + step].astype(jnp.float32)
                total += jnp.sum(part * hidden, axis=-1, keepdims=True)
            inverse = rms[rows, :][:, :1]
            back = (inverse * inverse * inverse) * (total / width)
            for n in range(0, width, step):
                hidden = act[rows, n : n + step].astype(jnp.float32)
                grad_input = inverse * scaled[:, n : n + step] - hidden * back
                c_out[b, :, n : n + step] = (
                    c_in[b, :, n : n + step].astype(jnp.float32) + grad_input
                ).astype(jnp.bfloat16)
            c_copy(b).start()

        return carry

    lax.fori_loop(0, BLOCKS, stage, 0)

    @pl.when(sec == SECTIONS - 1)
    def _():
        value_path()

    low = jnp.dot(
        c_in[...].reshape(LEN, width), gproj[...], preferred_element_type=jnp.float32
    )
    feat[...] = lax.dot_general(
        low, vlow[...], (((0,), (0,)), ((), ())),
        precision=lax.Precision.HIGHEST, preferred_element_type=jnp.float32,
    )
    for copy in started:
        copy.wait_send()

    @pl.when(sec > 0)
    def _():
        def sent(b, carry):
            c_copy(b).wait_send()
            return carry

        lax.fori_loop(0, BLOCKS, sent, 0)


def chain(act, top, mask, gain, vt_own, ot_own, vproj, gproj):
    tokens, width = act.shape
    kv = vt_own.shape[0]
    proj = vproj.shape[1]
    vmem = pl.BlockSpec(memory_space=pltpu.VMEM)
    dma = pltpu.SemaphoreType.DMA
    return pl.pallas_call(
        chain_kernel,
        out_shape=jax.ShapeDtypeStruct((proj, proj), jnp.float32),
        in_specs=[vmem] * 8,
        out_specs=vmem,
        scratch_shapes=[
            pltpu.VMEM((kv, width), jnp.bfloat16),
            pltpu.VMEM((width, kv), jnp.bfloat16),
            pltpu.VMEM((tokens, width), jnp.bfloat16),
            pltpu.VMEM((tokens, 128), jnp.float32),
            pltpu.VMEM((BLOCKS, ROWS, width), jnp.bfloat16),
            pltpu.VMEM((BLOCKS, ROWS, width), jnp.bfloat16),
            pltpu.VMEM((ROWS, width), jnp.float32),
            pltpu.VMEM((tokens, kv), jnp.bfloat16),
            pltpu.VMEM((tokens, proj), jnp.float32),
            dma((2, 4, 3)), dma((2, 4, 3)), dma((10,)), dma((10,)), dma((36,)), dma((36,)),
            dma((BLOCKS,)), dma((BLOCKS,)),
        ],
        compiler_params=pltpu.CompilerParams(
            collective_id=0, has_side_effects=True, vmem_limit_bytes=48 * 1024 * 1024
        ),
        cost_estimate=pl.CostEstimate(flops=3 * 10**9, bytes_accessed=4 * 10**6, transcendentals=0),
    )(act, top, mask, gain, vt_own, ot_own, vproj, gproj)


def per_device(
    activations, top_grad, loss_mask, norm_gain, value_weight, output_weight, value_proj, grad_proj, store
):
    feat = chain(
        activations[0], top_grad, loss_mask.reshape(1, -1), norm_gain, value_weight[0].T, output_weight[0].T,
        value_proj[0], grad_proj[0],
    )
    features = feat.reshape(1, -1)
    gathered = lax.all_gather(features, "shard", axis=0, tiled=True)
    scores = lax.dot_general(
        gathered, store[0], (((1,), (1,)), ((), ())),
        precision=lax.Precision.HIGHEST, preferred_element_type=jnp.float32,
    )
    count = lax.axis_size("section")
    blocks = scores.reshape(count, scores.shape[0] // count, scores.shape[1])
    arrived = lax.all_to_all(blocks, "section", split_axis=0, concat_axis=0, tiled=True)
    return arrived.sum(axis=0)


def solution(mesh):
    placed = (
        P("section", "shard", None),
        P("shard", None),
        P("shard"),
        P("section", None),
        P("section", "shard", None),
        P("section", None, "shard"),
        P("section", None, None),
        P("section", None, None),
        P("section", "shard", None),
    )
    return jax.shard_map(
        per_device, mesh=mesh, in_specs=placed, out_specs=P("section", "shard"), check_vma=False
    )
```

profile of v0, /device:TPU:7, one launch (start us, length us, event | category | flops | bytes accessed | tf_op | source)
XLA Modules:
  0.0 193.6 jit_solution(723720901129504440)
XLA Ops:
  0.0 0.0 copy-start
  0.0 0.0 copy-start.5
  0.0 0.0 copy-start.6
  0.0 1.9 copy.20
  1.9 1.8 copy.21
  3.7 1.1 copy.22
  4.8 1.6 copy.23
  6.4 0.0 copy-done.5
  6.4 0.0 copy-done.6
  6.5 0.0 copy-start.1
  6.5 0.9 copy-done.1
  7.4 0.0 copy-start.2
  7.4 0.9 copy-done.2
  8.4 1.1 copy-done.3
  9.5 1.1 copy-done.4
  10.6 111.0 %shard_map.91 = f32[64,64]{1,0:T(8,128)S(1)} custom-call(bf16[96,4096]{1,0:T(8,128)(2,1)S(1)} %bitcast.19, bf16[96,4096]{1,0:T(8,128)(2,1)S(1)} %copy-done.4, s32[1,96]{1,0:T(1,128)S(1)} %bitcast.20, f32[1,4096]{1,0:T(1,128)S(1)} %copy-done.5, bf16[1024,128]{1,0:T(8,128)(2,1)S(1)} %bitcast.17, bf16[128,1024]{1,0:T(8,128)(2,1)S(1)} %bitcast.18, ...), custom_call_target="tpu_custom_call" | custom-call | flops 3000000000 | bytes 4000000 | tf_op jit(solution)/shard_map/pallas_call | solution.py:285
  121.7 0.1 reshape.10
  121.7 34.2 %all-gather = f32[32,1,4096]{2,1,0:T(1,128)S(1)} all-gather(f32[1,1,4096]{2,1,0:T(1,128)S(1)} %reshape.10), channel_id=1, replica_groups=mesh['section'=8,'shard'=32] {'shard'}, dimensions={0}, use_global_device_ids=true | all-gather | bytes 540672 | tf_op jit(solution)/shard_map/all_gather | solution.py:318
  156.0 1.2 reduce
  157.2 0.1 dot_general.5
  157.4 0.0 copy-done
  157.4 2.3 %fusion = f32[8,4,128]{2,1,0:T(4,128)S(1)} fusion(f32[8,4,4096]{2,1,0:T(4,128)S(1)} %dot_general.5, f32[1,128,4096]{2,1,0:T(8,128)S(1)} %copy-done), kind=kOutput, calls=%fused_computation | convolution fusion | flops 201326592 | bytes 2637824 | tf_op jit(solution)/shard_map/dot_general | solution.py:319
  159.7 33.3 %all_to_all.5 = f32[8,4,128]{2,1,0:T(4,128)S(1)} all-to-all(f32[8,4,128]{2,1,0:T(4,128)S(1)} %fusion), channel_id=1, replica_groups=mesh['section'=8,'shard'=32] {'section'}, dimensions={0} | all-to-all | bytes 32768 | tf_op jit(solution)/shard_map/all_to_all | solution.py:325
  193.0 0.6 reduce_sum.9
  (2 shorter events, 0.0 us)
Async XLA Ops:
  0.0 157.4 %copy-start = (f32[1,128,4096]{2,1,0:T(8,128)S(1)}, f32[1,128,4096]{2,1,0:T(8,128)}, u32[]{:S(2)}) copy-start(f32[1,128,4096]{2,1,0:T(8,128)} %param.17) | copy-start | bytes 6291460
  0.0 6.4 %copy-start.5 = (f32[1,4096]{1,0:T(1,128)S(1)}, f32[1,4096]{1,0:T(1,128)}, u32[]{:S(2)}) copy-start(f32[1,4096]{1,0:T(1,128)} %gain.1) | copy-start | bytes 49156
  0.0 6.4 %copy-start.6 = (s32[96]{0:T(128)S(1)}, s32[96]{0:T(128)}, u32[]{:S(2)}) copy-start(s32[96]{0:T(128)} %param.11) | copy-start | bytes 1156
  6.5 1.0 copy-start.1
  7.4 0.9 copy-start.2
  8.4 1.1 copy-start.3
  9.5 1.1 copy-start.4
where the time goes:
time: 196 us; the launch traced here: 194 us
  Pallas kernels  111 us (57%)
  blocking collectives  67.5 us (34%)
  local copies, waits for them, and re-layouts  10.8 us (6%)
  matrix products  2.28 us (1%)
    pallas_call x1, Pallas kernels, chain(): pl.pallas_call(chain_kernel, out_shape=jax.ShapeDtypeStruct((proj, proj),...  111 us
    all_gather x1, blocking collectives, per_device(): gathered = lax.all_gather(features, 'shard', axis=0, tiled=True)  34.2 us
    all_to_all x1, blocking collectives, per_device(): lax.all_to_all(blocks, 'section', split_axis=0, concat_axis=0, tiled=True)  33.3 us
    unnamed x19, local copies, waits for them, and re-layouts  10.7 us

commit v1 on v0

--- a/solution.py
+++ b/solution.py
@@ -15,10 +15,12 @@
 
 
 def chain_kernel(
-    act, top, mask, gain, vt_own, ot_own, vproj, gproj,
-    feat,
+    act_hbm, top_hbm, mask, gain, v_hbm, o_hbm, vproj_hbm, gproj_hbm, store_hbm,
+    out,
+    act, top, vproj, gproj, store, v_raw, o_raw, vt_own, ot_own, store_low,
     wvt, wot, normed, rms, c_in, c_out, scaled, va, vlow,
-    zs, zr, xs, xr, ds_, dr, cs, cr,
+    feat, feat_own, feats, feat_rows, feat_all, part_out, part_in,
+    ls, zs, zr, xs, xr, ds_, dr, cs, cr, fs, fr, gs, gr, ps, pr,
 ):
     sec = lax.axis_index("section")
     shard = lax.axis_index("shard")
@@ -36,13 +38,28 @@
     z_prev = (z + NZ - 1) % NZ
     up = (sec + 1) % SECTIONS
     down = (sec + SECTIONS - 1) % SECTIONS
+    own_v = pltpu.make_async_copy(v_hbm, v_raw, ls.at[0])
+    own_o = pltpu.make_async_copy(o_hbm, o_raw, ls.at[1])
+    own_v.start()
+    own_o.start()
     barrier = pltpu.get_barrier_semaphore()
-    peers = (
-        dev(z_next, xl, core), dev(z_prev, xl, core), dev(z, 1 - xl, core), dev(z, xl, 1 - core),
-        (up, shard), (down, shard),
-    )
+    peers = [dev((z + p // 2) % NZ, (xl + p) % 2, core) for p in range(1, 2 * NZ)]
+    peers.append(dev(z, xl, 1 - core))
+    peers.extend([((sec + d) % SECTIONS, shard) for d in range(1, SECTIONS)])
     for peer in peers:
         pl.semaphore_signal(barrier, inc=1, device_id=peer, device_id_type=MESH)
+    local = [
+        pltpu.make_async_copy(source, target, ls.at[2 + n])
+        for n, (source, target) in enumerate(
+            ((act_hbm, act), (gproj_hbm, gproj), (vproj_hbm, vproj), (store_hbm, store), (top_hbm, top))
+        )
+    ]
+    for copy in local:
+        copy.start()
+    own_o.wait()
+    ot_own[...] = o_raw[...].T
+    own_v.wait()
+    vt_own[...] = v_raw[...].T
     pl.semaphore_wait(barrier, len(peers))
 
     def v_block(z_, x_, c_, half):
@@ -162,7 +179,9 @@
         normed[rows, :] = (hidden * inverse * gain[...]).astype(jnp.bfloat16)
         return carry
 
+    local[0].wait()
     lax.fori_loop(0, BLOCKS, prepare, 0)
+    local[4].wait()
 
     @pl.when(sec == SECTIONS - 1)
     def _():
@@ -177,10 +196,20 @@
 
         lax.fori_loop(0, BLOCKS, masked, 0)
 
+    local[1].wait()
+    local[2].wait()
+    local[3].wait()
+
+    def lowered(b, carry):
+        rows = pl.ds(pl.multiple_of(b * ROWS, ROWS), ROWS)
+        store_low[rows, :] = store[rows, :].astype(jnp.bfloat16)
+        return carry
+
     x_arrival(0).wait_recv()
     for direction in (0, 1):
         start(z_copy(direction, 0, 2))
     start(d_copy(26))
+    lax.fori_loop(0, store.shape[0] // ROWS, lowered, 0)
     x_arrival(1).wait_recv()
     start(d_copy(27))
     for k in range(4):
@@ -204,7 +233,9 @@
                 normed[...], wvt[n : n + 256, :], (((1,), (1,)), ((), ())), preferred_element_type=jnp.float32
             )
             va[:, n : n + 256] = part.astype(jnp.bfloat16)
-        vlow[...] = jnp.dot(va[...], vproj[...], preferred_element_type=jnp.float32)
+        vlow[...] = lax.dot_general(
+            va[...], vproj[...], (((1,), (1,)), ((), ())), preferred_element_type=jnp.float32
+        )
 
     def c_copy(b):
         return pltpu.make_async_remote_copy(
@@ -257,13 +288,92 @@
     def _():
         value_path()
 
-    low = jnp.dot(
-        c_in[...].reshape(LEN, width), gproj[...], preferred_element_type=jnp.float32
-    )
+    low = lax.dot_general(
+        c_in[...].reshape(LEN, width), gproj[...], (((1,), (1,)), ((), ())), preferred_element_type=jnp.float32
+    )
+    proj = low.shape[1]
+    half_rows = proj // 2
     feat[...] = lax.dot_general(
         low, vlow[...], (((0,), (0,)), ((), ())),
         precision=lax.Precision.HIGHEST, preferred_element_type=jnp.float32,
     )
+    even = feat[pl.ds(0, half_rows, stride=2), :]
+    odd = feat[pl.ds(1, half_rows, stride=2), :]
+    packed = jnp.concatenate([even, odd], axis=1).astype(jnp.bfloat16)
+    feat_own[...] = packed
+    feats[shard] = packed
+
+    def slot(p, c_):
+        return ((z + NZ - p // 2) % NZ) * 4 + ((xl + p) % 2) * 2 + c_
+
+    def f_copy(p):
+        return pltpu.make_async_remote_copy(
+            src_ref=feat_own, dst_ref=feats.at[shard], send_sem=fs.at[p], recv_sem=fr.at[p],
+            device_id=dev((z + p // 2) % NZ, (xl + p) % 2, core), device_id_type=MESH,
+        )
+
+    def f_arrival(p):
+        ref = feats.at[slot(p, core)]
+        return pltpu.make_async_remote_copy(
+            src_ref=ref, dst_ref=ref, send_sem=fs.at[p], recv_sem=fr.at[p],
+            device_id=dev((z + NZ - p // 2) % NZ, (xl + p) % 2, core), device_id_type=MESH,
+        )
+
+    def g_copy(p):
+        ref = feats.at[slot(p, core)]
+        return pltpu.make_async_remote_copy(
+            src_ref=feat_own if p == 0 else ref, dst_ref=ref, send_sem=gs.at[p], recv_sem=gr.at[p],
+            device_id=dev(z, xl, 1 - core), device_id_type=MESH,
+        )
+
+    def g_arrival(p):
+        ref = feats.at[slot(p, 1 - core)]
+        return pltpu.make_async_remote_copy(
+            src_ref=ref, dst_ref=ref, send_sem=gs.at[p], recv_sem=gr.at[p],
+            device_id=dev(z, xl, 1 - core), device_id_type=MESH,
+        )
+
+    near = (0, 1, 7, 2, 6, 3, 5, 4)
+    order = [2 * dz + dx for dz in near for dx in (0, 1)][1:]
+    for p in reversed(order):
+        start(f_copy(p))
+    start(g_copy(0))
+    for p in order:
+        f_arrival(p).wait_recv()
+        start(g_copy(p))
+    for p in [0] + order:
+        g_arrival(p).wait_recv()
+    gens = feats.shape[0]
+    for q in range(gens):
+        feat_rows[q * half_rows : (q + 1) * half_rows, :] = feats[q].astype(jnp.float32)
+    for i in range(half_rows):
+        feat_all[:, i * 128 : (i + 1) * 128] = feat_rows[pl.ds(i, gens, stride=half_rows), :].astype(jnp.bfloat16)
+    scores = lax.dot_general(
+        feat_all[...], store_low[...], (((1,), (1,)), ((), ())), preferred_element_type=jnp.float32
+    )
+    gens_each = gens // SECTIONS
+    for n in range(SECTIONS):
+        part_out[n] = scores[n * gens_each : (n + 1) * gens_each, :]
+
+    def p_copy(d):
+        return pltpu.make_async_remote_copy(
+            src_ref=part_out.at[(sec + d) % SECTIONS], dst_ref=part_in.at[d], send_sem=ps.at[d], recv_sem=pr.at[d],
+            device_id=((sec + d) % SECTIONS, shard), device_id_type=MESH,
+        )
+
+    def p_arrival(d):
+        return pltpu.make_async_remote_copy(
+            src_ref=part_in.at[d], dst_ref=part_in.at[d], send_sem=ps.at[d], recv_sem=pr.at[d],
+            device_id=((sec + SECTIONS - d) % SECTIONS, shard), device_id_type=MESH,
+        )
+
+    for d in range(1, SECTIONS):
+        start(p_copy(d))
+    total_scores = part_out[sec]
+    for d in range(1, SECTIONS):
+        p_arrival(d).wait_recv()
+        total_scores += part_in[d]
+    out[...] = total_scores
     for copy in started:
         copy.wait_send()
 
@@ -276,54 +386,67 @@
         lax.fori_loop(0, BLOCKS, sent, 0)
 
 
-def chain(act, top, mask, gain, vt_own, ot_own, vproj, gproj):
+def chain(act, top, mask, gain, v_own, o_own, vproj, gproj, store):
     tokens, width = act.shape
-    kv = vt_own.shape[0]
-    proj = vproj.shape[1]
+    kv = v_own.shape[1]
+    proj = vproj.shape[0]
+    examples = store.shape[0]
+    gens = NZ * 4
     vmem = pl.BlockSpec(memory_space=pltpu.VMEM)
+    hbm = pl.BlockSpec(memory_space=pltpu.HBM)
     dma = pltpu.SemaphoreType.DMA
+    bf16, f32 = jnp.bfloat16, jnp.float32
     return pl.pallas_call(
         chain_kernel,
-        out_shape=jax.ShapeDtypeStruct((proj, proj), jnp.float32),
-        in_specs=[vmem] * 8,
+        out_shape=jax.ShapeDtypeStruct((gens // SECTIONS, examples), f32),
+        in_specs=[hbm, hbm, vmem, vmem] + [hbm] * 5,
         out_specs=vmem,
         scratch_shapes=[
-            pltpu.VMEM((kv, width), jnp.bfloat16),
-            pltpu.VMEM((width, kv), jnp.bfloat16),
-            pltpu.VMEM((tokens, width), jnp.bfloat16),
-            pltpu.VMEM((tokens, 128), jnp.float32),
-            pltpu.VMEM((BLOCKS, ROWS, width), jnp.bfloat16),
-            pltpu.VMEM((BLOCKS, ROWS, width), jnp.bfloat16),
-            pltpu.VMEM((ROWS, width), jnp.float32),
-            pltpu.VMEM((tokens, kv), jnp.bfloat16),
-            pltpu.VMEM((tokens, proj), jnp.float32),
+            pltpu.VMEM(act.shape, bf16),
+            pltpu.VMEM(top.shape, bf16),
+            pltpu.VMEM(vproj.shape, bf16),
+            pltpu.VMEM(gproj.shape, bf16),
+            pltpu.VMEM(store.shape, f32),
+            pltpu.VMEM(v_own.shape, bf16),
+            pltpu.VMEM(o_own.shape, bf16),
+            pltpu.VMEM(v_own.shape[::-1], bf16),
+            pltpu.VMEM(o_own.shape[::-1], bf16),
+            pltpu.VMEM(store.shape, bf16),
+            pltpu.VMEM((kv, width), bf16),
+            pltpu.VMEM((width, kv), bf16),
+            pltpu.VMEM((tokens, width), bf16),
+            pltpu.VMEM((tokens, 128), f32),
+            pltpu.VMEM((BLOCKS, ROWS, width), bf16),
+            pltpu.VMEM((BLOCKS, ROWS, width), bf16),
+            pltpu.VMEM((ROWS, width), f32),
+            pltpu.VMEM((tokens, kv), bf16),
+            pltpu.VMEM((tokens, proj), f32),
+            pltpu.VMEM((proj, proj), f32),
+            pltpu.VMEM((proj // 2, 2 * proj), bf16),
+            pltpu.VMEM((gens, proj // 2, 2 * proj), bf16),
+            pltpu.VMEM((gens * proj // 2, 2 * proj), f32),
+            pltpu.VMEM((gens, proj * proj), bf16),
+            pltpu.VMEM((SECTIONS, gens // SECTIONS, examples), f32),
+            pltpu.VMEM((SECTIONS, gens // SECTIONS, examples), f32),
+            dma((7,)),
             dma((2, 4, 3)), dma((2, 4, 3)), dma((10,)), dma((10,)), dma((36,)), dma((36,)),
             dma((BLOCKS,)), dma((BLOCKS,)),
+            dma((2 * NZ,)), dma((2 * NZ,)), dma((2 * NZ,)), dma((2 * NZ,)), dma((SECTIONS,)), dma((SECTIONS,)),
         ],
         compiler_params=pltpu.CompilerParams(
-            collective_id=0, has_side_effects=True, vmem_limit_bytes=48 * 1024 * 1024
+            collective_id=0, has_side_effects=True, vmem_limit_bytes=60 * 1024 * 1024
         ),
         cost_estimate=pl.CostEstimate(flops=3 * 10**9, bytes_accessed=4 * 10**6, transcendentals=0),
-    )(act, top, mask, gain, vt_own, ot_own, vproj, gproj)
+    )(act, top, mask, gain, v_own, o_own, vproj, gproj, store)
 
 
 def per_device(
     activations, top_grad, loss_mask, norm_gain, value_weight, output_weight, value_proj, grad_proj, store
 ):
-    feat = chain(
-        activations[0], top_grad, loss_mask.reshape(1, -1), norm_gain, value_weight[0].T, output_weight[0].T,
-        value_proj[0], grad_proj[0],
-    )
-    features = feat.reshape(1, -1)
-    gathered = lax.all_gather(features, "shard", axis=0, tiled=True)
-    scores = lax.dot_general(
-        gathered, store[0], (((1,), (1,)), ((), ())),
-        precision=lax.Precision.HIGHEST, preferred_element_type=jnp.float32,
-    )
-    count = lax.axis_size("section")
-    blocks = scores.reshape(count, scores.shape[0] // count, scores.shape[1])
-    arrived = lax.all_to_all(blocks, "section", split_axis=0, concat_axis=0, tiled=True)
-    return arrived.sum(axis=0)
+    return chain(
+        activations[0], top_grad, loss_mask.reshape(1, -1), norm_gain, value_weight[0], output_weight[0],
+        value_proj[0].T, grad_proj[0].T, store[0],
+    )
 
 
 def solution(mesh):

time: 196 us -> 153 us (0.78); the launches traced: 194 us -> 153 us
  blocking collectives: 67.5 us -> 0 us
  Pallas kernels: 111 us -> 151 us
  local copies, waits for them, and re-layouts: 10.8 us -> 1.26 us
  matrix products: 2.28 us -> 0 us
    pallas_call x1, Pallas kernels: 111 us -> 151 us  [chain(): pl.pallas_call(chain_kernel, out_shape=jax.ShapeDtypeStruct((gens // SECT...]
    all_gather x1 -> x0, blocking collectives: 34.2 us -> none  [per_device(): gathered = lax.all_gather(features, 'shard', axis=0, tiled=True)]
    all_to_all x1 -> x0, blocking collectives: 33.3 us -> none  [per_device(): lax.all_to_all(blocks, 'section', split_axis=0, concat_axis=0, tiled=True)]
    unnamed x19 -> x1, local copies, waits for them, and re-layouts: 10.7 us -> 1.26 us
    dot_general x1 -> x0, matrix products: 2.28 us -> none  [per_device(): lax.dot_general(gathered, store[0], (((1,), (1,)), ((), ())), precision=l...]
where the time goes in v1:
time: 153 us
  Pallas kernels  151 us (99%)
    pallas_call x1, Pallas kernels, chain(): pl.pallas_call(chain_kernel, out_shape=jax.ShapeDtypeStruct((gens // SECT...  151 us

profile of v1, /device:TPU:7, one launch (start us, length us, event | category | flops | bytes accessed | tf_op | source)
XLA Modules:
  0.0 152.6 jit_solution(15207814860370910103)
XLA Ops:
  0.0 151.3 %shard_map.91 = f32[4,128]{1,0:T(4,128)} custom-call(bf16[96,4096]{1,0:T(8,128)(2,1)} %bitcast.12, bf16[96,4096]{1,0:T(8,128)(2,1)} %top_hbm.1, s32[1,96]{1,0:T(1,128)} %bitcast.17, f32[1,4096]{1,0:T(1,128)} %gain.1, bf16[128,1024]{1,0:T(8,128)(2,1)} %bitcast.14, bf16[1024,128]{1,0:T(8,128)(2,1)} %bitcast.15, bf16[64,1024]{1,0:T(8,128)(2,1)} %bitcast.16, ...), custom_call_target="tpu_custom_call" | custom-call | flops 3000000000 | bytes 4000000 | tf_op jit(solution)/shard_map/pallas_call | solution.py:399
  151.3 1.3 copy.11

commit v2 on v1

--- a/solution.py
+++ b/solution.py
@@ -12,15 +12,16 @@
 SECTIONS = 8
 ROWS = 16
 BLOCKS = LEN // ROWS
+PIECES = 4
 
 
 def chain_kernel(
     act_hbm, top_hbm, mask, gain, v_hbm, o_hbm, vproj_hbm, gproj_hbm, store_hbm,
     out,
     act, top, vproj, gproj, store, v_raw, o_raw, vt_own, ot_own, store_low,
-    wvt, wot, normed, rms, c_in, c_out, scaled, va, vlow,
+    wvt, wot, held, normed, rms, c_in, c_out, va_sum, va, vlow,
     feat, feat_own, feats, feat_rows, feat_all, part_out, part_in,
-    ls, zs, zr, xs, xr, ds_, dr, cs, cr, fs, fr, gs, gr, ps, pr,
+    ls, zs, zr, xs, xr, ds_, dr, hs, hr, cs, cr, fs, fr, gs, gr, ps, pr,
 ):
     sec = lax.axis_index("section")
     shard = lax.axis_index("shard")
@@ -44,6 +45,8 @@
     own_o.start()
     barrier = pltpu.get_barrier_semaphore()
     peers = [dev((z + p // 2) % NZ, (xl + p) % 2, core) for p in range(1, 2 * NZ)]
+    outer = ((sec + SECTIONS // 2) % SECTIONS, z * 4 + (1 - xl) * 2 + core)
+    peers.append(outer)
     peers.append(dev(z, xl, 1 - core))
     peers.extend([((sec + d) % SECTIONS, shard) for d in range(1, SECTIONS)])
     for peer in peers:
@@ -68,41 +71,54 @@
             return wvt.at[:, pl.ds(first, cols)]
         return wvt.at[pl.ds(half * (kv // 2), kv // 2), pl.ds(first, cols)]
 
-    def o_block(z_, x_, c_, half):
-        first = (z_ * 4 + x_ * 2 + c_) * cols
-        if half is None:
-            return wot.at[pl.ds(pl.multiple_of(first, cols), cols), :]
-        return wot.at[pl.ds(pl.multiple_of(first + half * (cols // 2), cols // 2), cols // 2), :]
-
-    def block(item, z_, c_, half):
+    def o_block(z_, x_, c_, span):
+        begin, size = span
+        first = pl.multiple_of((z_ * 4 + x_ * 2 + c_) * cols + begin, 16)
+        return wot.at[pl.ds(first, size), :]
+
+    def o_span(item, k, direction, client):
+        begin, size = 0, cols
+        if item == 3 or (item == 1 and client):
+            size = cols // 2
+            begin = 0 if item == 3 else cols // 2
+        if k == 3:
+            size = size // 2
+            begin += direction * size
+        return begin, size
+
+    def block(item, z_, c_, k, direction, client):
         if item == 0:
-            return v_block(z_, xl, c_, half)
-        return o_block(z_, xl if item == 1 else 1 - xl, c_, half)
+            return v_block(z_, xl, c_, None if k < 3 else direction)
+        span = o_span(item, k, direction, client)
+        if item == 3:
+            return held.at[z_, pl.ds(*span), :]
+        return o_block(z_, xl if item == 1 else 1 - xl, c_, span)
 
     def origin(direction, hops):
         return (z + (NZ - hops if direction == 0 else hops)) % NZ
 
-    def z_copy(direction, k, item):
-        half = None if k < 3 else direction
-        zo = origin(direction, k)
-        dst = block(item, zo, core, half)
-        src = (vt_own if item == 0 else ot_own) if k == 0 and item < 2 else dst
-        return pltpu.make_async_remote_copy(
-            src_ref=src, dst_ref=dst, send_sem=zs.at[direction, k, item], recv_sem=zr.at[direction, k, item],
-            device_id=dev(z_next if direction == 0 else z_prev, xl, core), device_id_type=MESH,
-        )
-
-    def z_arrival(direction, k, item):
-        half = None if k < 3 else direction
-        ref = block(item, origin(direction, k + 1), core, half)
-        return pltpu.make_async_remote_copy(
-            src_ref=ref, dst_ref=ref, send_sem=zs.at[direction, k, item], recv_sem=zr.at[direction, k, item],
-            device_id=dev(z_prev if direction == 0 else z_next, xl, core), device_id_type=MESH,
-        )
+    def remote(src, dst, sends, recvs, index, peer):
+        return pltpu.make_async_remote_copy(
+            src_ref=src, dst_ref=dst, send_sem=sends.at[index], recv_sem=recvs.at[index],
+            device_id=peer, device_id_type=MESH,
+        )
+
+    def z_copy(direction, k, item, client):
+        dst = block(item, origin(direction, k), core, k, direction, client)
+        src = dst
+        if k == 0 and item == 0:
+            src = vt_own
+        if k == 0 and item == 1:
+            src = ot_own.at[pl.ds(*o_span(1, 0, direction, client)), :]
+        return remote(src, dst, zs, zr, (direction, k, item), dev(z_next if direction == 0 else z_prev, xl, core))
+
+    def z_arrival(direction, k, item, client):
+        ref = block(item, origin(direction, k + 1), core, k, direction, client)
+        return remote(ref, ref, zs, zr, (direction, k, item), dev(z_prev if direction == 0 else z_next, xl, core))
 
     def x_refs(index, x_):
         if index == 0:
-            return o_block(z, x_, core, None)
+            return o_block(z, x_, core, (0, cols))
         if index == 1:
             return v_block(z, x_, core, None)
         direction, k = (index - 2) // 4, (index - 2) % 4
@@ -110,63 +126,176 @@
 
     def x_copy(index):
         dst = x_refs(index, xl)
-        src = (ot_own, vt_own)[index] if index < 2 else dst
-        return pltpu.make_async_remote_copy(
-            src_ref=src, dst_ref=dst, send_sem=xs.at[index], recv_sem=xr.at[index],
-            device_id=dev(z, 1 - xl, core), device_id_type=MESH,
-        )
+        return remote((ot_own, vt_own)[index] if index < 2 else dst, dst, xs, xr, index, dev(z, 1 - xl, core))
 
     def x_arrival(index):
         ref = x_refs(index, 1 - xl)
-        return pltpu.make_async_remote_copy(
-            src_ref=ref, dst_ref=ref, send_sem=xs.at[index], recv_sem=xr.at[index],
-            device_id=dev(z, 1 - xl, core), device_id_type=MESH,
-        )
-
-    def d_refs(index, c_):
+        return remote(ref, ref, xs, xr, index, dev(z, 1 - xl, core))
+
+    def d_refs(index, c_, client):
         if index == 0:
-            return o_block(z, xl, c_, None)
+            return o_block(z, xl, c_, (0, cols))
         if index == 1:
             return v_block(z, xl, c_, None)
         if index < 26:
             direction, k, item = (index - 2) // 12, (index - 2) // 3 % 4, (index - 2) % 3
-            return block(item, origin(direction, k + 1), c_, None if k < 3 else direction)
-        index -= 26
-        if index == 0:
-            return o_block(z, 1 - xl, c_, None)
-        if index == 1:
+            return block(item, origin(direction, k + 1), c_, k, direction, client)
+        if index == 26:
+            return o_block(z, 1 - xl, c_, (0, cols))
+        if index == 27:
             return v_block(z, 1 - xl, c_, None)
-        direction, k = (index - 2) // 4, (index - 2) % 4
-        return v_block(origin(direction, k + 1), 1 - xl, c_, None if k < 3 else direction)
-
-    def d_copy(index):
-        dst = d_refs(index, core)
-        src = (ot_own, vt_own)[index] if index < 2 else dst
-        return pltpu.make_async_remote_copy(
-            src_ref=src, dst_ref=dst, send_sem=ds_.at[index], recv_sem=dr.at[index],
-            device_id=dev(z, xl, 1 - core), device_id_type=MESH,
-        )
-
-    def d_arrival(index):
-        ref = d_refs(index, 1 - core)
-        return pltpu.make_async_remote_copy(
-            src_ref=ref, dst_ref=ref, send_sem=ds_.at[index], recv_sem=dr.at[index],
-            device_id=dev(z, xl, 1 - core), device_id_type=MESH,
-        )
-
-    started = []
-
-    def start(copy):
-        copy.start()
-        started.append(copy)
-
-    start(x_copy(0))
-    start(x_copy(1))
-    for item in (0, 1):
+        if index < 36:
+            direction, k = (index - 28) // 4, (index - 28) % 4
+            return v_block(origin(direction, k + 1), 1 - xl, c_, None if k < 3 else direction)
+        direction, k = (index - 36) // 4, (index - 36) % 4
+        return o_block(origin(direction, k + 1), xl, c_, o_span(3, k, direction, client))
+
+    def d_copy(index, client):
+        dst = d_refs(index, core, client)
+        return remote((ot_own, vt_own)[index] if index < 2 else dst, dst, ds_, dr, index, dev(z, xl, 1 - core))
+
+    def d_arrival(index, client):
+        ref = d_refs(index, 1 - core, client)
+        return remote(ref, ref, ds_, dr, index, dev(z, xl, 1 - core))
+
+    def lent_copy():
+        return remote(ot_own.at[pl.ds(0, cols // 2), :], held.at[z], hs, hr, 0, outer)
+
+    def lent_arrival():
+        return remote(held.at[z], held.at[z], hs, hr, 0, outer)
+
+    def back_copy(direction, k):
+        zo = origin(direction, k + 1)
+        span = o_span(3, k, direction, True)
+        return remote(
+            held.at[zo, pl.ds(*span), :], o_block(zo, 1 - xl, core, span), hs, hr, 1 + direction * 4 + k, outer
+        )
+
+    def back_arrival(direction, k):
+        ref = o_block(origin(direction, k + 1), xl, core, o_span(3, k, direction, True))
+        return remote(ref, ref, hs, hr, 1 + direction * 4 + k, outer)
+
+    started = {True: [], False: [], None: []}
+
+    def start(role, make, *given):
+        make(*given).start()
+        started[role].append((make, given))
+
+    def value_pair(z_, x_):
+        span = pl.ds(pl.multiple_of((z_ * 4 + x_ * 2) * cols, 2 * cols), 2 * cols)
+        left = normed[:, span]
+        for n in range(0, kv, 256):
+            va_sum[:, n : n + 256] += lax.dot_general(
+                left, wvt[n : n + 256, span], (((1,), (1,)), ((), ())), preferred_element_type=jnp.float32
+            )
+
+    def pairs_of(k, client):
+        if k < 0:
+            for index in (1, 27):
+                d_arrival(index, client).wait_recv()
+            value_pair(z, 0)
+            value_pair(z, 1)
+            return
         for direction in (0, 1):
-            start(z_copy(direction, 0, item))
-    start(d_copy(0))
-    start(d_copy(1))
+            d_arrival(2 + direction * 12 + k * 3, client).wait_recv()
+            d_arrival(28 + direction * 4 + k, client).wait_recv()
+            if k < 3 or direction == 1:
+                value_pair(origin(direction, k + 1), 0)
+                value_pair(origin(direction, k + 1), 1)
+
+    def begin(client):
+        start(client, x_copy, 0)
+        start(client, x_copy, 1)
+        if client:
+            start(client, lent_copy)
+        for item in (0, 1) if client else (0,):
+            for direction in (0, 1):
+                start(client, z_copy, direction, 0, item, client)
+        start(client, d_copy, 0, client)
+        start(client, d_copy, 1, client)
+
+    def z_step(direction, k, item, client):
+        z_arrival(direction, k, item, client).wait_recv()
+        if k < 3:
+            start(client, z_copy, direction, k + 1, item, client)
+        if item == 0:
+            start(client, x_copy, 2 + direction * 4 + k)
+        if item == 3:
+            start(client, back_copy, direction, k)
+        else:
+            start(client, d_copy, 2 + direction * 12 + k * 3 + item, client)
+
+    def x_step(k, client):
+        for direction in (0, 1):
+            x_arrival(2 + direction * 4 + k).wait_recv()
+            start(client, d_copy, 28 + direction * 4 + k, client)
+
+    def last_waits(client):
+        pairs_of(3, client)
+        late = [0, 26] + [2 + direction * 12 + k * 3 + item for direction in (0, 1) for k in range(4) for item in (1, 2)]
+        if client:
+            late += range(36, 44)
+        for index in late:
+            d_arrival(index, client).wait_recv()
+
+    def gather_client():
+        x_arrival(0).wait_recv()
+        for direction in (0, 1):
+            start(True, z_copy, direction, 0, 2, True)
+        start(True, d_copy, 26, True)
+        x_arrival(1).wait_recv()
+        start(True, d_copy, 27, True)
+        for k in range(4):
+            for item in (0, 1):
+                for direction in (0, 1):
+                    z_step(direction, k, item, True)
+            if k == 3:
+                x_step(k, True)
+                pairs_of(k - 1, True)
+            for direction in (0, 1):
+                back_arrival(direction, k).wait_recv()
+                start(True, d_copy, 36 + direction * 4 + k, True)
+            for direction in (0, 1):
+                z_step(direction, k, 2, True)
+            if k < 3:
+                x_step(k, True)
+                pairs_of(k - 1, True)
+        last_waits(True)
+
+    def gather_helper():
+        lent_arrival().wait_recv()
+        for direction in (0, 1):
+            start(False, z_copy, direction, 0, 3, False)
+        x_arrival(0).wait_recv()
+        start(False, d_copy, 26, False)
+        for k in range(4):
+            if k == 3:
+                for item in (1, 2):
+                    for direction in (0, 1):
+                        start(False, z_copy, direction, 0, item, False)
+            for item in (0, 3):
+                for direction in (0, 1):
+                    z_step(direction, k, item, False)
+        x_arrival(1).wait_recv()
+        start(False, d_copy, 27, False)
+        for k in range(4):
+            for item in (1, 2):
+                for direction in (0, 1):
+                    z_step(direction, k, item, False)
+            x_step(k, False)
+            pairs_of(k - 1, False)
+        last_waits(False)
+
+    half_of = SECTIONS // 2
+
+    @pl.when(sec >= half_of)
+    def _():
+        begin(True)
+
+    @pl.when(sec < half_of)
+    def _():
+        begin(False)
+
     own = pl.ds(pl.multiple_of(shard * cols, cols), cols)
     wvt[:, own] = vt_own[...]
     wot[own, :] = ot_own[...]
@@ -205,80 +334,73 @@
         store_low[rows, :] = store[rows, :].astype(jnp.bfloat16)
         return carry
 
-    x_arrival(0).wait_recv()
-    for direction in (0, 1):
-        start(z_copy(direction, 0, 2))
-    start(d_copy(26))
     lax.fori_loop(0, store.shape[0] // ROWS, lowered, 0)
-    x_arrival(1).wait_recv()
-    start(d_copy(27))
-    for k in range(4):
-        for item in range(3):
-            for direction in (0, 1):
-                z_arrival(direction, k, item).wait_recv()
-                if k < 3:
-                    start(z_copy(direction, k + 1, item))
-                if item == 0:
-                    start(x_copy(2 + direction * 4 + k))
-                start(d_copy(2 + direction * 12 + k * 3 + item))
-        for direction in (0, 1):
-            x_arrival(2 + direction * 4 + k).wait_recv()
-            start(d_copy(26 + 2 + direction * 4 + k))
-    for index in range(36):
-        d_arrival(index).wait_recv()
+    va_sum[...] = jnp.zeros_like(va_sum)
+
+    @pl.when(sec >= half_of)
+    def _():
+        gather_client()
+
+    @pl.when(sec < half_of)
+    def _():
+        gather_helper()
 
     def value_path():
-        for n in range(0, kv, 256):
-            part = lax.dot_general(
-                normed[...], wvt[n : n + 256, :], (((1,), (1,)), ((), ())), preferred_element_type=jnp.float32
-            )
-            va[:, n : n + 256] = part.astype(jnp.bfloat16)
+        va[...] = va_sum[...].astype(jnp.bfloat16)
         vlow[...] = lax.dot_general(
             va[...], vproj[...], (((1,), (1,)), ((), ())), preferred_element_type=jnp.float32
         )
 
-    def c_copy(b):
-        return pltpu.make_async_remote_copy(
-            src_ref=c_out.at[b], dst_ref=c_in.at[b], send_sem=cs.at[b], recv_sem=cr.at[b],
+    piece = width // PIECES
+
+    def c_copy(b, n):
+        span = pl.ds(n * piece, piece)
+        return pltpu.make_async_remote_copy(
+            src_ref=c_out.at[b, :, span], dst_ref=c_in.at[b, :, span], send_sem=cs.at[b, n], recv_sem=cr.at[b, n],
             device_id=(down, shard), device_id_type=MESH,
         )
 
-    def c_arrival(b):
-        return pltpu.make_async_remote_copy(
-            src_ref=c_in.at[b], dst_ref=c_in.at[b], send_sem=cs.at[b], recv_sem=cr.at[b],
+    def c_arrival(b, n):
+        ref = c_in.at[b, :, pl.ds(n * piece, piece)]
+        return pltpu.make_async_remote_copy(
+            src_ref=ref, dst_ref=ref, send_sem=cs.at[b, n], recv_sem=cr.at[b, n],
             device_id=(up, shard), device_id_type=MESH,
         )
 
-    @pl.when(sec < SECTIONS - 1)
-    def _():
-        value_path()
-
-    def stage(b, carry):
+    def arrived(b, pieces):
         @pl.when(sec < SECTIONS - 1)
         def _():
-            c_arrival(b).wait_recv()
+            for n in pieces:
+                c_arrival(b, n).wait_recv()
+
+    @pl.when(sec < SECTIONS - 1)
+    def _():
+        value_path()
+
+    def stage(b, carry):
+        @pl.when(sec == 0)
+        def _():
+            arrived(b, range(PIECES))
 
         @pl.when(sec > 0)
         def _():
             rows = pl.ds(pl.multiple_of(b * ROWS, ROWS), ROWS)
-            grad_value = jnp.dot(c_in[b], wot[...], preferred_element_type=jnp.float32).astype(jnp.bfloat16)
-            total = jnp.zeros((ROWS, 1), jnp.float32)
-            step = 512
-            for n in range(0, width, step):
-                part = jnp.dot(grad_value, wvt[:, n : n + step], preferred_element_type=jnp.float32)
-                part = gain[:, n : n + step] * part
-                scaled[:, n : n + step] = part
-                hidden = act[rows, n : n + step].astype(jnp.float32)
-                total += jnp.sum(part * hidden, axis=-1, keepdims=True)
+            split = width - piece
+            arrived(b, range(PIECES - 1))
+            grad_value = jnp.dot(c_in[b, :, :split], wot[:split, :], preferred_element_type=jnp.float32)
+            arrived(b, (PIECES - 1,))
+            grad_value += jnp.dot(c_in[b, :, split:], wot[split:, :], preferred_element_type=jnp.float32)
+            grad_value = grad_value.astype(jnp.bfloat16)
             inverse = rms[rows, :][:, :1]
-            back = (inverse * inverse * inverse) * (total / width)
-            for n in range(0, width, step):
-                hidden = act[rows, n : n + step].astype(jnp.float32)
-                grad_input = inverse * scaled[:, n : n + step] - hidden * back
-                c_out[b, :, n : n + step] = (
-                    c_in[b, :, n : n + step].astype(jnp.float32) + grad_input
-                ).astype(jnp.bfloat16)
-            c_copy(b).start()
+            total = jnp.sum(grad_value.astype(jnp.float32) * va_sum[rows, :], axis=-1, keepdims=True)
+            back = (inverse * inverse) * (total / width)
+            for n in range(PIECES):
+                span = slice(n * piece, (n + 1) * piece)
+                part = gain[:, span] * jnp.dot(grad_value, wvt[:, span], preferred_element_type=jnp.float32)
+                hidden = act[rows, span].astype(jnp.float32)
+                grad_input = inverse * part - hidden * back
+                c_out[b, :, span] = (c_in[b, :, span].astype(jnp.float32) + grad_input).astype(jnp.bfloat16)
+                c_copy(b, n).start()
 
         return carry
 
@@ -336,11 +458,11 @@
     near = (0, 1, 7, 2, 6, 3, 5, 4)
     order = [2 * dz + dx for dz in near for dx in (0, 1)][1:]
     for p in reversed(order):
-        start(f_copy(p))
-    start(g_copy(0))
+        start(None, f_copy, p)
+    start(None, g_copy, 0)
     for p in order:
         f_arrival(p).wait_recv()
-        start(g_copy(p))
+        start(None, g_copy, p)
     for p in [0] + order:
         g_arrival(p).wait_recv()
     gens = feats.shape[0]
@@ -368,19 +490,30 @@
         )
 
     for d in range(1, SECTIONS):
-        start(p_copy(d))
+        start(None, p_copy, d)
     total_scores = part_out[sec]
     for d in range(1, SECTIONS):
         p_arrival(d).wait_recv()
         total_scores += part_in[d]
     out[...] = total_scores
-    for copy in started:
-        copy.wait_send()
+    for make, given in started[None]:
+        make(*given).wait_send()
+
+    @pl.when(sec >= half_of)
+    def _():
+        for make, given in started[True]:
+            make(*given).wait_send()
+
+    @pl.when(sec < half_of)
+    def _():
+        for make, given in started[False]:
+            make(*given).wait_send()
 
     @pl.when(sec > 0)
     def _():
         def sent(b, carry):
-            c_copy(b).wait_send()
+            for n in range(PIECES):
+                c_copy(b, n).wait_send()
             return carry
 
         lax.fori_loop(0, BLOCKS, sent, 0)
@@ -414,11 +547,12 @@
             pltpu.VMEM(store.shape, bf16),
             pltpu.VMEM((kv, width), bf16),
             pltpu.VMEM((width, kv), bf16),
+            pltpu.VMEM((NZ, v_own.shape[0] // 2, kv), bf16),
             pltpu.VMEM((tokens, width), bf16),
             pltpu.VMEM((tokens, 128), f32),
             pltpu.VMEM((BLOCKS, ROWS, width), bf16),
             pltpu.VMEM((BLOCKS, ROWS, width), bf16),
-            pltpu.VMEM((ROWS, width), f32),
+            pltpu.VMEM((tokens, kv), f32),
             pltpu.VMEM((tokens, kv), bf16),
             pltpu.VMEM((tokens, proj), f32),
             pltpu.VMEM((proj, proj), f32),
@@ -429,8 +563,8 @@
             pltpu.VMEM((SECTIONS, gens // SECTIONS, examples), f32),
             pltpu.VMEM((SECTIONS, gens // SECTIONS, examples), f32),
             dma((7,)),
-            dma((2, 4, 3)), dma((2, 4, 3)), dma((10,)), dma((10,)), dma((36,)), dma((36,)),
-            dma((BLOCKS,)), dma((BLOCKS,)),
+            dma((2, 4, 4)), dma((2, 4, 4)), dma((10,)), dma((10,)), dma((44,)), dma((44,)), dma((9,)), dma((9,)),
+            dma((BLOCKS, PIECES)), dma((BLOCKS, PIECES)),
             dma((2 * NZ,)), dma((2 * NZ,)), dma((2 * NZ,)), dma((2 * NZ,)), dma((SECTIONS,)), dma((SECTIONS,)),
         ],
         compiler_params=pltpu.CompilerParams(

time: 153 us -> 142 us (0.928)
  Pallas kernels: 151 us -> 140 us
    pallas_call x1, Pallas kernels: 151 us -> 140 us  [chain(): pl.pallas_call(chain_kernel, out_shape=jax.ShapeDtypeStruct((gens // SECT...]
where the time goes in v2:
time: 142 us
  Pallas kernels  140 us (99%)
    pallas_call x1, Pallas kernels, chain(): pl.pallas_call(chain_kernel, out_shape=jax.ShapeDtypeStruct((gens // SECT...  140 us

profile of v2, /device:TPU:7, one launch (start us, length us, event | category | flops | bytes accessed | tf_op | source)
XLA Modules:
  0.0 141.5 jit_solution(8711168879281606015)
XLA Ops:
  0.0 140.3 %shard_map.91 = f32[4,128]{1,0:T(4,128)} custom-call(bf16[96,4096]{1,0:T(8,128)(2,1)} %bitcast.12, bf16[96,4096]{1,0:T(8,128)(2,1)} %top_hbm.1, s32[1,96]{1,0:T(1,128)} %bitcast.17, f32[1,4096]{1,0:T(1,128)} %gain.1, bf16[128,1024]{1,0:T(8,128)(2,1)} %bitcast.14, bf16[1024,128]{1,0:T(8,128)(2,1)} %bitcast.15, bf16[64,1024]{1,0:T(8,128)(2,1)} %bitcast.16, ...), custom_call_target="tpu_custom_call" | custom-call | flops 3000000000 | bytes 4000000 | tf_op jit(solution)/shard_map/pallas_call | solution.py:532
  140.3 1.3 copy.11

commit v3 on v2

--- a/solution.py
+++ b/solution.py
@@ -13,6 +13,7 @@
 ROWS = 16
 BLOCKS = LEN // ROWS
 PIECES = 4
+GROUPS = ((0, 3), (3, 4))
 
 
 def chain_kernel(
@@ -99,7 +100,7 @@
 
     def remote(src, dst, sends, recvs, index, peer):
         return pltpu.make_async_remote_copy(
-            src_ref=src, dst_ref=dst, send_sem=sends.at[index], recv_sem=recvs.at[index],
+            src_ref=src, dst_ref=dst, send_sem=sends.at[0], recv_sem=recvs.at[index],
             device_id=peer, device_id_type=MESH,
         )
 
@@ -150,13 +151,27 @@
         direction, k = (index - 36) // 4, (index - 36) % 4
         return o_block(origin(direction, k + 1), xl, c_, o_span(3, k, direction, client))
 
+    def d_group(index):
+        if index in (1, 27):
+            return 1
+        if 2 <= index < 26 and (index - 2) % 3 == 0:
+            return 2 + (index - 2) // 3 % 4
+        if 28 <= index < 36:
+            return 2 + (index - 28) % 4
+        return 0
+
     def d_copy(index, client):
         dst = d_refs(index, core, client)
-        return remote((ot_own, vt_own)[index] if index < 2 else dst, dst, ds_, dr, index, dev(z, xl, 1 - core))
-
-    def d_arrival(index, client):
-        ref = d_refs(index, 1 - core, client)
-        return remote(ref, ref, ds_, dr, index, dev(z, xl, 1 - core))
+        src = (ot_own, vt_own)[index] if index < 2 else dst
+        return remote(src, dst, ds_, dr, d_group(index), dev(z, xl, 1 - core))
+
+    def d_arrivals(group):
+        units = {0: 16, 1: 2, 5: 2}.get(group, 4)
+        ref = wot.at[pl.ds(0, units * cols), :]
+        return remote(ref, ref, ds_, dr, group, dev(z, xl, 1 - core))
+
+    def all_sent(sends, ref):
+        remote(ref, ref, sends, dr, 0, dev(z, xl, 1 - core)).wait_send()
 
     def lent_copy():
         return remote(ot_own.at[pl.ds(0, cols // 2), :], held.at[z], hs, hr, 0, outer)
@@ -174,12 +189,6 @@
     def back_arrival(direction, k):
         ref = o_block(origin(direction, k + 1), xl, core, o_span(3, k, direction, True))
         return remote(ref, ref, hs, hr, 1 + direction * 4 + k, outer)
-
-    started = {True: [], False: [], None: []}
-
-    def start(role, make, *given):
-        make(*given).start()
-        started[role].append((make, given))
 
     def value_pair(z_, x_):
         span = pl.ds(pl.multiple_of((z_ * 4 + x_ * 2) * cols, 2 * cols), 2 * cols)
@@ -190,94 +199,84 @@
             )
 
     def pairs_of(k, client):
-        if k < 0:
-            for index in (1, 27):
-                d_arrival(index, client).wait_recv()
-            value_pair(z, 0)
-            value_pair(z, 1)
-            return
+        d_arrivals(2 + k).wait_recv()
         for direction in (0, 1):
-            d_arrival(2 + direction * 12 + k * 3, client).wait_recv()
-            d_arrival(28 + direction * 4 + k, client).wait_recv()
-            if k < 3 or direction == 1:
+            if 0 <= k < 3 or direction == 1:
                 value_pair(origin(direction, k + 1), 0)
                 value_pair(origin(direction, k + 1), 1)
 
     def begin(client):
-        start(client, x_copy, 0)
-        start(client, x_copy, 1)
+        x_copy(0).start()
+        x_copy(1).start()
         if client:
-            start(client, lent_copy)
+            lent_copy().start()
         for item in (0, 1) if client else (0,):
             for direction in (0, 1):
-                start(client, z_copy, direction, 0, item, client)
-        start(client, d_copy, 0, client)
-        start(client, d_copy, 1, client)
+                z_copy(direction, 0, item, client).start()
+        d_copy(0, client).start()
+        d_copy(1, client).start()
 
     def z_step(direction, k, item, client):
         z_arrival(direction, k, item, client).wait_recv()
         if k < 3:
-            start(client, z_copy, direction, k + 1, item, client)
+            z_copy(direction, k + 1, item, client).start()
         if item == 0:
-            start(client, x_copy, 2 + direction * 4 + k)
+            x_copy(2 + direction * 4 + k).start()
         if item == 3:
-            start(client, back_copy, direction, k)
+            back_copy(direction, k).start()
         else:
-            start(client, d_copy, 2 + direction * 12 + k * 3 + item, client)
+            d_copy(2 + direction * 12 + k * 3 + item, client).start()
 
     def x_step(k, client):
         for direction in (0, 1):
             x_arrival(2 + direction * 4 + k).wait_recv()
-            start(client, d_copy, 28 + direction * 4 + k, client)
+            d_copy(28 + direction * 4 + k, client).start()
 
     def last_waits(client):
         pairs_of(3, client)
-        late = [0, 26] + [2 + direction * 12 + k * 3 + item for direction in (0, 1) for k in range(4) for item in (1, 2)]
-        if client:
-            late += range(36, 44)
-        for index in late:
-            d_arrival(index, client).wait_recv()
+        d_arrivals(0).wait_recv()
 
     def gather_client():
         x_arrival(0).wait_recv()
         for direction in (0, 1):
-            start(True, z_copy, direction, 0, 2, True)
-        start(True, d_copy, 26, True)
-        x_arrival(1).wait_recv()
-        start(True, d_copy, 27, True)
+            z_copy(direction, 0, 2, True).start()
+        d_copy(26, True).start()
         for k in range(4):
             for item in (0, 1):
                 for direction in (0, 1):
                     z_step(direction, k, item, True)
-            if k == 3:
-                x_step(k, True)
-                pairs_of(k - 1, True)
+            if k == 0:
+                x_arrival(1).wait_recv()
+                d_copy(27, True).start()
+            else:
+                x_step(k - 1, True)
             for direction in (0, 1):
                 back_arrival(direction, k).wait_recv()
-                start(True, d_copy, 36 + direction * 4 + k, True)
+                d_copy(36 + direction * 4 + k, True).start()
             for direction in (0, 1):
                 z_step(direction, k, 2, True)
-            if k < 3:
-                x_step(k, True)
-                pairs_of(k - 1, True)
+            if k > 0:
+                pairs_of(k - 2, True)
+        pairs_of(2, True)
+        x_step(3, True)
         last_waits(True)
 
     def gather_helper():
         lent_arrival().wait_recv()
         for direction in (0, 1):
-            start(False, z_copy, direction, 0, 3, False)
+            z_copy(direction, 0, 3, False).start()
         x_arrival(0).wait_recv()
-        start(False, d_copy, 26, False)
+        d_copy(26, False).start()
         for k in range(4):
             if k == 3:
                 for item in (1, 2):
                     for direction in (0, 1):
-                        start(False, z_copy, direction, 0, item, False)
+                        z_copy(direction, 0, item, False).start()
             for item in (0, 3):
                 for direction in (0, 1):
                     z_step(direction, k, item, False)
         x_arrival(1).wait_recv()
-        start(False, d_copy, 27, False)
+        d_copy(27, False).start()
         for k in range(4):
             for item in (1, 2):
                 for direction in (0, 1):
@@ -355,116 +354,150 @@
 
     def c_copy(b, n):
         span = pl.ds(n * piece, piece)
-        return pltpu.make_async_remote_copy(
-            src_ref=c_out.at[b, :, span], dst_ref=c_in.at[b, :, span], send_sem=cs.at[b, n], recv_sem=cr.at[b, n],
+        group = [first <= n < last for first, last in GROUPS].index(True)
+        return pltpu.make_async_remote_copy(
+            src_ref=c_out.at[b, :, span], dst_ref=c_in.at[b, :, span], send_sem=cs.at[0], recv_sem=cr.at[b, group],
             device_id=(down, shard), device_id_type=MESH,
         )
 
-    def c_arrival(b, n):
-        ref = c_in.at[b, :, pl.ds(n * piece, piece)]
-        return pltpu.make_async_remote_copy(
-            src_ref=ref, dst_ref=ref, send_sem=cs.at[b, n], recv_sem=cr.at[b, n],
+    def arrived(b, group):
+        first, last = GROUPS[group]
+        ref = c_in.at[b, :, pl.ds(first * piece, (last - first) * piece)]
+        pltpu.make_async_remote_copy(
+            src_ref=ref, dst_ref=ref, send_sem=cs.at[0], recv_sem=cr.at[b, group],
             device_id=(up, shard), device_id_type=MESH,
-        )
-
-    def arrived(b, pieces):
-        @pl.when(sec < SECTIONS - 1)
+        ).wait_recv()
+
+    half_rows = gproj.shape[0] // 2
+
+    def features():
+        low = lax.dot_general(
+            c_in[...].reshape(LEN, width), gproj[...], (((1,), (1,)), ((), ())), preferred_element_type=jnp.float32
+        )
+        feat[...] = lax.dot_general(
+            low, vlow[...], (((0,), (0,)), ((), ())),
+            precision=lax.Precision.HIGHEST, preferred_element_type=jnp.float32,
+        )
+        even = feat[pl.ds(0, half_rows, stride=2), :]
+        odd = feat[pl.ds(1, half_rows, stride=2), :]
+        packed = jnp.concatenate([even, odd], axis=1).astype(jnp.bfloat16)
+        feat_own[...] = packed
+        feats[shard] = packed
+
+    @pl.when(sec < SECTIONS - 1)
+    def _():
+        value_path()
+
+    def stage(b, top_layer):
+        rows = pl.ds(pl.multiple_of(b * ROWS, ROWS), ROWS)
+        grad_value = jnp.zeros((ROWS, kv), jnp.float32)
+        for group, (first, last) in enumerate(GROUPS):
+            if not top_layer:
+                arrived(b, group)
+            span = slice(first * piece, last * piece)
+            grad_value += jnp.dot(c_in[b, :, span], wot[span, :], preferred_element_type=jnp.float32)
+        grad_value = grad_value.astype(jnp.bfloat16)
+        inverse = rms[rows, :][:, :1]
+        total = jnp.sum(grad_value.astype(jnp.float32) * va_sum[rows, :], axis=-1, keepdims=True)
+        back = (inverse * inverse) * (total / width)
+        for n in range(PIECES):
+            span = slice(n * piece, (n + 1) * piece)
+            part = gain[:, span] * jnp.dot(grad_value, wvt[:, span], preferred_element_type=jnp.float32)
+            hidden = act[rows, span].astype(jnp.float32)
+            grad_input = inverse * part - hidden * back
+            c_out[b, :, span] = (c_in[b, :, span].astype(jnp.float32) + grad_input).astype(jnp.bfloat16)
+            c_copy(b, n).start()
+
+    def stages(top_layer):
+        def one(b, carry):
+            stage(b, top_layer)
+            return carry
+
+        lax.fori_loop(0, BLOCKS, one, 0)
+
+    def rows_of(units):
+        return wot.at[pl.ds(0, units * cols // 2), :]
+
+    def settle():
+        @pl.when(sec >= half_of)
         def _():
-            for n in pieces:
-                c_arrival(b, n).wait_recv()
+            all_sent(zs, rows_of(35))
+            all_sent(hs, rows_of(1))
+
+        @pl.when(sec < half_of)
+        def _():
+            all_sent(zs, rows_of(49))
+            all_sent(hs, rows_of(7))
+
+        all_sent(xs, rows_of(18))
+        all_sent(ds_, rows_of(64))
 
     @pl.when(sec < SECTIONS - 1)
     def _():
+        settle()
+
+    @pl.when(sec == 0)
+    def _():
+        def one(b, carry):
+            for group in range(len(GROUPS)):
+                arrived(b, group)
+            return carry
+
+        lax.fori_loop(0, BLOCKS, one, 0)
+
+    @pl.when((sec > 0) & (sec < SECTIONS - 1))
+    def _():
+        stages(False)
+
+    @pl.when(sec == SECTIONS - 1)
+    def _():
+        stages(True)
+
+    @pl.when(sec == SECTIONS - 1)
+    def _():
         value_path()
 
-    def stage(b, carry):
-        @pl.when(sec == 0)
-        def _():
-            arrived(b, range(PIECES))
-
-        @pl.when(sec > 0)
-        def _():
-            rows = pl.ds(pl.multiple_of(b * ROWS, ROWS), ROWS)
-            split = width - piece
-            arrived(b, range(PIECES - 1))
-            grad_value = jnp.dot(c_in[b, :, :split], wot[:split, :], preferred_element_type=jnp.float32)
-            arrived(b, (PIECES - 1,))
-            grad_value += jnp.dot(c_in[b, :, split:], wot[split:, :], preferred_element_type=jnp.float32)
-            grad_value = grad_value.astype(jnp.bfloat16)
-            inverse = rms[rows, :][:, :1]
-            total = jnp.sum(grad_value.astype(jnp.float32) * va_sum[rows, :], axis=-1, keepdims=True)
-            back = (inverse * inverse) * (total / width)
-            for n in range(PIECES):
-                span = slice(n * piece, (n + 1) * piece)
-                part = gain[:, span] * jnp.dot(grad_value, wvt[:, span], preferred_element_type=jnp.float32)
-                hidden = act[rows, span].astype(jnp.float32)
-                grad_input = inverse * part - hidden * back
-                c_out[b, :, span] = (c_in[b, :, span].astype(jnp.float32) + grad_input).astype(jnp.bfloat16)
-                c_copy(b, n).start()
-
-        return carry
-
-    lax.fori_loop(0, BLOCKS, stage, 0)
-
-    @pl.when(sec == SECTIONS - 1)
-    def _():
-        value_path()
-
-    low = lax.dot_general(
-        c_in[...].reshape(LEN, width), gproj[...], (((1,), (1,)), ((), ())), preferred_element_type=jnp.float32
-    )
-    proj = low.shape[1]
-    half_rows = proj // 2
-    feat[...] = lax.dot_general(
-        low, vlow[...], (((0,), (0,)), ((), ())),
-        precision=lax.Precision.HIGHEST, preferred_element_type=jnp.float32,
-    )
-    even = feat[pl.ds(0, half_rows, stride=2), :]
-    odd = feat[pl.ds(1, half_rows, stride=2), :]
-    packed = jnp.concatenate([even, odd], axis=1).astype(jnp.bfloat16)
-    feat_own[...] = packed
-    feats[shard] = packed
+    features()
 
     def slot(p, c_):
         return ((z + NZ - p // 2) % NZ) * 4 + ((xl + p) % 2) * 2 + c_
 
     def f_copy(p):
         return pltpu.make_async_remote_copy(
-            src_ref=feat_own, dst_ref=feats.at[shard], send_sem=fs.at[p], recv_sem=fr.at[p],
+            src_ref=feat_own, dst_ref=feats.at[shard], send_sem=fs.at[0], recv_sem=fr.at[p],
             device_id=dev((z + p // 2) % NZ, (xl + p) % 2, core), device_id_type=MESH,
         )
 
     def f_arrival(p):
         ref = feats.at[slot(p, core)]
         return pltpu.make_async_remote_copy(
-            src_ref=ref, dst_ref=ref, send_sem=fs.at[p], recv_sem=fr.at[p],
+            src_ref=ref, dst_ref=ref, send_sem=fs.at[0], recv_sem=fr.at[p],
             device_id=dev((z + NZ - p // 2) % NZ, (xl + p) % 2, core), device_id_type=MESH,
         )
 
     def g_copy(p):
         ref = feats.at[slot(p, core)]
         return pltpu.make_async_remote_copy(
-            src_ref=feat_own if p == 0 else ref, dst_ref=ref, send_sem=gs.at[p], recv_sem=gr.at[p],
+            src_ref=feat_own if p == 0 else ref, dst_ref=ref, send_sem=gs.at[0], recv_sem=gr.at[0],
             device_id=dev(z, xl, 1 - core), device_id_type=MESH,
         )
 
-    def g_arrival(p):
-        ref = feats.at[slot(p, 1 - core)]
-        return pltpu.make_async_remote_copy(
-            src_ref=ref, dst_ref=ref, send_sem=gs.at[p], recv_sem=gr.at[p],
+    def g_arrivals():
+        ref = feats.at[pl.ds(0, 2 * NZ)]
+        return pltpu.make_async_remote_copy(
+            src_ref=ref, dst_ref=ref, send_sem=gs.at[0], recv_sem=gr.at[0],
             device_id=dev(z, xl, 1 - core), device_id_type=MESH,
         )
 
     near = (0, 1, 7, 2, 6, 3, 5, 4)
     order = [2 * dz + dx for dz in near for dx in (0, 1)][1:]
     for p in reversed(order):
-        start(None, f_copy, p)
-    start(None, g_copy, 0)
+        f_copy(p).start()
+    g_copy(0).start()
     for p in order:
         f_arrival(p).wait_recv()
-        start(None, g_copy, p)
-    for p in [0] + order:
-        g_arrival(p).wait_recv()
+        g_copy(p).start()
+    g_arrivals().wait_recv()
     gens = feats.shape[0]
     for q in range(gens):
         feat_rows[q * half_rows : (q + 1) * half_rows, :] = feats[q].astype(jnp.float32)
@@ -479,44 +512,36 @@
 
     def p_copy(d):
         return pltpu.make_async_remote_copy(
-            src_ref=part_out.at[(sec + d) % SECTIONS], dst_ref=part_in.at[d], send_sem=ps.at[d], recv_sem=pr.at[d],
+            src_ref=part_out.at[(sec + d) % SECTIONS], dst_ref=part_in.at[d], send_sem=ps.at[0], recv_sem=pr.at[0],
             device_id=((sec + d) % SECTIONS, shard), device_id_type=MESH,
         )
 
-    def p_arrival(d):
-        return pltpu.make_async_remote_copy(
-            src_ref=part_in.at[d], dst_ref=part_in.at[d], send_sem=ps.at[d], recv_sem=pr.at[d],
-            device_id=((sec + SECTIONS - d) % SECTIONS, shard), device_id_type=MESH,
+    def p_arrivals():
+        ref = part_in.at[pl.ds(1, SECTIONS - 1)]
+        return pltpu.make_async_remote_copy(
+            src_ref=ref, dst_ref=ref, send_sem=ps.at[0], recv_sem=pr.at[0],
+            device_id=(down, shard), device_id_type=MESH,
         )
 
     for d in range(1, SECTIONS):
-        start(None, p_copy, d)
+        p_copy(d).start()
+    all_sent(fs, feats.at[pl.ds(0, 2 * NZ - 1)])
+    all_sent(gs, feats.at[pl.ds(0, 2 * NZ)])
+
+    @pl.when(sec > 0)
+    def _():
+        all_sent(cs, c_out)
+
+    @pl.when(sec == SECTIONS - 1)
+    def _():
+        settle()
+
     total_scores = part_out[sec]
+    p_arrivals().wait_recv()
     for d in range(1, SECTIONS):
-        p_arrival(d).wait_recv()
         total_scores += part_in[d]
+    p_arrivals().wait_send()
     out[...] = total_scores
-    for make, given in started[None]:
-        make(*given).wait_send()
-
-    @pl.when(sec >= half_of)
-    def _():
-        for make, given in started[True]:
-            make(*given).wait_send()
-
-    @pl.when(sec < half_of)
-    def _():
-        for make, given in started[False]:
-            make(*given).wait_send()
-
-    @pl.when(sec > 0)
-    def _():
-        def sent(b, carry):
-            for n in range(PIECES):
-                c_copy(b, n).wait_send()
-            return carry
-
-        lax.fori_loop(0, BLOCKS, sent, 0)
 
 
 def chain(act, top, mask, gain, v_own, o_own, vproj, gproj, store):
@@ -563,9 +588,9 @@
             pltpu.VMEM((SECTIONS, gens // SECTIONS, examples), f32),
             pltpu.VMEM((SECTIONS, gens // SECTIONS, examples), f32),
             dma((7,)),
-            dma((2, 4, 4)), dma((2, 4, 4)), dma((10,)), dma((10,)), dma((44,)), dma((44,)), dma((9,)), dma((9,)),
-            dma((BLOCKS, PIECES)), dma((BLOCKS, PIECES)),
-            dma((2 * NZ,)), dma((2 * NZ,)), dma((2 * NZ,)), dma((2 * NZ,)), dma((SECTIONS,)), dma((SECTIONS,)),
+            dma((1,)), dma((2, 4, 4)), dma((1,)), dma((10,)), dma((1,)), dma((6,)), dma((1,)), dma((9,)),
+            dma((1,)), dma((BLOCKS, len(GROUPS))),
+            dma((1,)), dma((2 * NZ,)), dma((1,)), dma((1,)), dma((1,)), dma((1,)),
         ],
         compiler_params=pltpu.CompilerParams(
             collective_id=0, has_side_effects=True, vmem_limit_bytes=60 * 1024 * 1024

time: 142 us -> 138 us (0.972)
  Pallas kernels: 140 us -> 136 us
    pallas_call x1, Pallas kernels: 140 us -> 136 us  [chain(): pl.pallas_call(chain_kernel, out_shape=jax.ShapeDtypeStruct((gens // SECT...]
where the time goes in v3:
time: 138 us; the launch traced here: 137 us
  Pallas kernels  136 us (99%)
    pallas_call x1, Pallas kernels, chain(): pl.pallas_call(chain_kernel, out_shape=jax.ShapeDtypeStruct((gens // SECT...  136 us

profile of v3, /device:TPU:7, one launch (start us, length us, event | category | flops | bytes accessed | tf_op | source)
XLA Modules:
  0.0 137.5 jit_solution(14212821282752399081)
XLA Ops:
  0.0 136.2 %shard_map.91 = f32[4,128]{1,0:T(4,128)} custom-call(bf16[96,4096]{1,0:T(8,128)(2,1)} %bitcast.12, bf16[96,4096]{1,0:T(8,128)(2,1)} %top_hbm.1, s32[1,96]{1,0:T(1,128)} %bitcast.17, f32[1,4096]{1,0:T(1,128)} %gain.1, bf16[128,1024]{1,0:T(8,128)(2,1)} %bitcast.14, bf16[1024,128]{1,0:T(8,128)(2,1)} %bitcast.15, bf16[64,1024]{1,0:T(8,128)(2,1)} %bitcast.16, ...), custom_call_target="tpu_custom_call" | custom-call | flops 3000000000 | bytes 4000000 | tf_op jit(solution)/shard_map/pallas_call | solution.py:557
  136.2 1.3 copy.11

commit v4 on v3

--- a/solution.py
+++ b/solution.py
@@ -72,16 +72,24 @@
             return wvt.at[:, pl.ds(first, cols)]
         return wvt.at[pl.ds(half * (kv // 2), kv // 2), pl.ds(first, cols)]
 
+    def v_rows(z_, x_, c_, begin, size):
+        first = pl.multiple_of((z_ * 4 + x_ * 2 + c_) * cols, cols)
+        return wvt.at[pl.ds(begin, size), pl.ds(first, cols)]
+
     def o_block(z_, x_, c_, span):
         begin, size = span
         first = pl.multiple_of((z_ * 4 + x_ * 2 + c_) * cols + begin, 16)
         return wot.at[pl.ds(first, size), :]
 
+    lent = cols * 3 // 4
+    side = kv // 8
+
     def o_span(item, k, direction, client):
         begin, size = 0, cols
-        if item == 3 or (item == 1 and client):
-            size = cols // 2
-            begin = 0 if item == 3 else cols // 2
+        if item == 3:
+            size = lent
+        if item == 1 and client:
+            begin, size = lent, cols - lent
         if k == 3:
             size = size // 2
             begin += direction * size
@@ -90,6 +98,8 @@
     def block(item, z_, c_, k, direction, client):
         if item == 0:
             return v_block(z_, xl, c_, None if k < 3 else direction)
+        if item == 4:
+            return v_rows(z_, 1 - xl, c_, *((0, side) if k < 3 else (direction * side // 2, side // 2)))
         span = o_span(item, k, direction, client)
         if item == 3:
             return held.at[z_, pl.ds(*span), :]
@@ -117,20 +127,26 @@
         ref = block(item, origin(direction, k + 1), core, k, direction, client)
         return remote(ref, ref, zs, zr, (direction, k, item), dev(z_prev if direction == 0 else z_next, xl, core))
 
-    def x_refs(index, x_):
+    def x_forward(z_, x_, c_, direction, k, client):
+        begin, end = (0, kv) if k < 3 else (direction * (kv // 2), (direction + 1) * (kv // 2))
+        if client:
+            begin = max(begin, side)
+        return v_rows(z_, x_, c_, begin, end - begin)
+
+    def x_refs(index, x_, client):
         if index == 0:
             return o_block(z, x_, core, (0, cols))
         if index == 1:
             return v_block(z, x_, core, None)
         direction, k = (index - 2) // 4, (index - 2) % 4
-        return v_block(origin(direction, k + 1), x_, core, None if k < 3 else direction)
-
-    def x_copy(index):
-        dst = x_refs(index, xl)
+        return x_forward(origin(direction, k + 1), x_, core, direction, k, client)
+
+    def x_copy(index, client):
+        dst = x_refs(index, xl, client)
         return remote((ot_own, vt_own)[index] if index < 2 else dst, dst, xs, xr, index, dev(z, 1 - xl, core))
 
-    def x_arrival(index):
-        ref = x_refs(index, 1 - xl)
+    def x_arrival(index, client):
+        ref = x_refs(index, 1 - xl, client)
         return remote(ref, ref, xs, xr, index, dev(z, 1 - xl, core))
 
     def d_refs(index, c_, client):
@@ -147,7 +163,10 @@
             return v_block(z, 1 - xl, c_, None)
         if index < 36:
             direction, k = (index - 28) // 4, (index - 28) % 4
-            return v_block(origin(direction, k + 1), 1 - xl, c_, None if k < 3 else direction)
+            return x_forward(origin(direction, k + 1), 1 - xl, c_, direction, k, client)
+        if index >= 44:
+            direction, k = (index - 44) // 4, (index - 44) % 4
+            return block(4, origin(direction, k + 1), c_, k, direction, client)
         direction, k = (index - 36) // 4, (index - 36) % 4
         return o_block(origin(direction, k + 1), xl, c_, o_span(3, k, direction, client))
 
@@ -158,6 +177,8 @@
             return 2 + (index - 2) // 3 % 4
         if 28 <= index < 36:
             return 2 + (index - 28) % 4
+        if index >= 44:
+            return 2 + (index - 44) % 4
         return 0
 
     def d_copy(index, client):
@@ -174,7 +195,7 @@
         remote(ref, ref, sends, dr, 0, dev(z, xl, 1 - core)).wait_send()
 
     def lent_copy():
-        return remote(ot_own.at[pl.ds(0, cols // 2), :], held.at[z], hs, hr, 0, outer)
+        return remote(ot_own.at[pl.ds(0, lent), :], held.at[z], hs, hr, 0, outer)
 
     def lent_arrival():
         return remote(held.at[z], held.at[z], hs, hr, 0, outer)
@@ -206,8 +227,8 @@
                 value_pair(origin(direction, k + 1), 1)
 
     def begin(client):
-        x_copy(0).start()
-        x_copy(1).start()
+        x_copy(0, client).start()
+        x_copy(1, client).start()
         if client:
             lent_copy().start()
         for item in (0, 1) if client else (0,):
@@ -221,15 +242,17 @@
         if k < 3:
             z_copy(direction, k + 1, item, client).start()
         if item == 0:
-            x_copy(2 + direction * 4 + k).start()
+            x_copy(2 + direction * 4 + k, client).start()
         if item == 3:
             back_copy(direction, k).start()
+        elif item == 4:
+            d_copy(44 + direction * 4 + k, client).start()
         else:
             d_copy(2 + direction * 12 + k * 3 + item, client).start()
 
     def x_step(k, client):
         for direction in (0, 1):
-            x_arrival(2 + direction * 4 + k).wait_recv()
+            x_arrival(2 + direction * 4 + k, client).wait_recv()
             d_copy(28 + direction * 4 + k, client).start()
 
     def last_waits(client):
@@ -237,7 +260,7 @@
         d_arrivals(0).wait_recv()
 
     def gather_client():
-        x_arrival(0).wait_recv()
+        x_arrival(0, True).wait_recv()
         for direction in (0, 1):
             z_copy(direction, 0, 2, True).start()
         d_copy(26, True).start()
@@ -246,15 +269,18 @@
                 for direction in (0, 1):
                     z_step(direction, k, item, True)
             if k == 0:
-                x_arrival(1).wait_recv()
+                x_arrival(1, True).wait_recv()
                 d_copy(27, True).start()
+                for direction in (0, 1):
+                    z_copy(direction, 0, 4, True).start()
             else:
                 x_step(k - 1, True)
             for direction in (0, 1):
                 back_arrival(direction, k).wait_recv()
                 d_copy(36 + direction * 4 + k, True).start()
-            for direction in (0, 1):
-                z_step(direction, k, 2, True)
+            for item in (2, 4):
+                for direction in (0, 1):
+                    z_step(direction, k, item, True)
             if k > 0:
                 pairs_of(k - 2, True)
         pairs_of(2, True)
@@ -265,7 +291,7 @@
         lent_arrival().wait_recv()
         for direction in (0, 1):
             z_copy(direction, 0, 3, False).start()
-        x_arrival(0).wait_recv()
+        x_arrival(0, False).wait_recv()
         d_copy(26, False).start()
         for k in range(4):
             if k == 3:
@@ -275,7 +301,7 @@
             for item in (0, 3):
                 for direction in (0, 1):
                     z_step(direction, k, item, False)
-        x_arrival(1).wait_recv()
+        x_arrival(1, False).wait_recv()
         d_copy(27, False).start()
         for k in range(4):
             for item in (1, 2):
@@ -388,14 +414,19 @@
     def _():
         value_path()
 
-    def stage(b, top_layer):
+    def stage(b, top_layer, eager):
         rows = pl.ds(pl.multiple_of(b * ROWS, ROWS), ROWS)
-        grad_value = jnp.zeros((ROWS, kv), jnp.float32)
-        for group, (first, last) in enumerate(GROUPS):
+        if eager:
+            grad_value = jnp.zeros((ROWS, kv), jnp.float32)
+            for group, (first, last) in enumerate(GROUPS):
+                arrived(b, group)
+                span = slice(first * piece, last * piece)
+                grad_value += jnp.dot(c_in[b, :, span], wot[span, :], preferred_element_type=jnp.float32)
+        else:
             if not top_layer:
-                arrived(b, group)
-            span = slice(first * piece, last * piece)
-            grad_value += jnp.dot(c_in[b, :, span], wot[span, :], preferred_element_type=jnp.float32)
+                for group in range(len(GROUPS)):
+                    arrived(b, group)
+            grad_value = jnp.dot(c_in[b], wot[...], preferred_element_type=jnp.float32)
         grad_value = grad_value.astype(jnp.bfloat16)
         inverse = rms[rows, :][:, :1]
         total = jnp.sum(grad_value.astype(jnp.float32) * va_sum[rows, :], axis=-1, keepdims=True)
@@ -410,27 +441,33 @@
 
     def stages(top_layer):
         def one(b, carry):
-            stage(b, top_layer)
+            stage(b, top_layer, False)
             return carry
 
-        lax.fori_loop(0, BLOCKS, one, 0)
-
-    def rows_of(units):
-        return wot.at[pl.ds(0, units * cols // 2), :]
+        if not top_layer:
+            stage(0, False, True)
+        lax.fori_loop(0 if top_layer else 1, BLOCKS, one, 0)
+
+    def rows_of(count):
+        return wot.at[pl.ds(0, count), :]
 
     def settle():
+        wide = 7 * cols
+        moved = side * cols // kv
+
         @pl.when(sec >= half_of)
         def _():
-            all_sent(zs, rows_of(35))
-            all_sent(hs, rows_of(1))
+            all_sent(zs, rows_of(2 * wide + 7 * (cols - lent) + 7 * moved))
+            all_sent(hs, rows_of(lent))
+            all_sent(xs, rows_of(2 * cols + wide - 7 * moved))
 
         @pl.when(sec < half_of)
         def _():
-            all_sent(zs, rows_of(49))
-            all_sent(hs, rows_of(7))
-
-        all_sent(xs, rows_of(18))
-        all_sent(ds_, rows_of(64))
+            all_sent(zs, rows_of(3 * wide + 7 * lent))
+            all_sent(hs, rows_of(7 * lent))
+            all_sent(xs, rows_of(2 * cols + wide))
+
+        all_sent(ds_, rows_of(4 * wide + 4 * cols))
 
     @pl.when(sec < SECTIONS - 1)
     def _():
@@ -536,12 +573,10 @@
     def _():
         settle()
 
-    total_scores = part_out[sec]
+    part_in[0] = part_out[sec]
+    p_arrivals().wait_send()
     p_arrivals().wait_recv()
-    for d in range(1, SECTIONS):
-        total_scores += part_in[d]
-    p_arrivals().wait_send()
-    out[...] = total_scores
+    out[...] = part_in[...]
 
 
 def chain(act, top, mask, gain, v_own, o_own, vproj, gproj, store):
@@ -556,7 +591,7 @@
     bf16, f32 = jnp.bfloat16, jnp.float32
     return pl.pallas_call(
         chain_kernel,
-        out_shape=jax.ShapeDtypeStruct((gens // SECTIONS, examples), f32),
+        out_shape=jax.ShapeDtypeStruct((SECTIONS, gens // SECTIONS, examples), f32),
         in_specs=[hbm, hbm, vmem, vmem] + [hbm] * 5,
         out_specs=vmem,
         scratch_shapes=[
@@ -572,7 +607,7 @@
             pltpu.VMEM(store.shape, bf16),
             pltpu.VMEM((kv, width), bf16),
             pltpu.VMEM((width, kv), bf16),
-            pltpu.VMEM((NZ, v_own.shape[0] // 2, kv), bf16),
+            pltpu.VMEM((NZ, v_own.shape[0] * 3 // 4, kv), bf16),
             pltpu.VMEM((tokens, width), bf16),
             pltpu.VMEM((tokens, 128), f32),
             pltpu.VMEM((BLOCKS, ROWS, width), bf16),
@@ -588,7 +623,7 @@
             pltpu.VMEM((SECTIONS, gens // SECTIONS, examples), f32),
             pltpu.VMEM((SECTIONS, gens // SECTIONS, examples), f32),
             dma((7,)),
-            dma((1,)), dma((2, 4, 4)), dma((1,)), dma((10,)), dma((1,)), dma((6,)), dma((1,)), dma((9,)),
+            dma((1,)), dma((2, 4, 5)), dma((1,)), dma((10,)), dma((1,)), dma((6,)), dma((1,)), dma((9,)),
             dma((1,)), dma((BLOCKS, len(GROUPS))),
             dma((1,)), dma((2 * NZ,)), dma((1,)), dma((1,)), dma((1,)), dma((1,)),
         ],
@@ -602,10 +637,11 @@
 def per_device(
     activations, top_grad, loss_mask, norm_gain, value_weight, output_weight, value_proj, grad_proj, store
 ):
-    return chain(
+    parts = chain(
         activations[0], top_grad, loss_mask.reshape(1, -1), norm_gain, value_weight[0], output_weight[0],
         value_proj[0].T, grad_proj[0].T, store[0],
     )
+    return parts.sum(axis=0)
 
 
 def solution(mesh):

time: 138 us -> 135 us (0.978)
  Pallas kernels: 136 us -> 134 us
    pallas_call x1, Pallas kernels: 136 us -> 134 us  [chain(): pl.pallas_call(chain_kernel, out_shape=jax.ShapeDtypeStruct((SECTIONS, ge...]
where the time goes in v4:
time: 135 us
  Pallas kernels  134 us (99%)
    pallas_call x1, Pallas kernels, chain(): pl.pallas_call(chain_kernel, out_shape=jax.ShapeDtypeStruct((SECTIONS, ge...  134 us

profile of v4, /device:TPU:7, one launch (start us, length us, event | category | flops | bytes accessed | tf_op | source)
XLA Modules:
  0.0 135.1 jit_solution(1484111358097311179)
XLA Ops:
  0.0 133.8 %shard_map.91 = f32[8,4,128]{2,1,0:T(4,128)} custom-call(bf16[96,4096]{1,0:T(8,128)(2,1)} %bitcast.12, bf16[96,4096]{1,0:T(8,128)(2,1)} %top_hbm.1, s32[1,96]{1,0:T(1,128)} %bitcast.17, f32[1,4096]{1,0:T(1,128)} %gain.1, bf16[128,1024]{1,0:T(8,128)(2,1)} %bitcast.14, bf16[1024,128]{1,0:T(8,128)(2,1)} %bitcast.15, bf16[64,1024]{1,0:T(8,128)(2,1)} %bitcast.16, ...), custom_call_target="tpu_custom_call" | custom-call | flops 3000000000 | bytes 4000000 | tf_op jit(solution)/shard_map/pallas_call | solution.py:592
  133.8 1.3 reduce_sum.9

commit v5 on v4

--- a/solution.py
+++ b/solution.py
@@ -21,8 +21,8 @@
     out,
     act, top, vproj, gproj, store, v_raw, o_raw, vt_own, ot_own, store_low,
     wvt, wot, held, normed, rms, c_in, c_out, va_sum, va, vlow,
-    feat, feat_own, feats, feat_rows, feat_all, part_out, part_in,
-    ls, zs, zr, xs, xr, ds_, dr, hs, hr, cs, cr, fs, fr, gs, gr, ps, pr,
+    feat, feat_own, gproj_in, vlow_in, feat_in, feats, feat_rows, feat_all, part_out, part_in,
+    ls, zs, zr, xs, xr, ds_, dr, hs, hr, cs, cr, fs, fr, gs, gr, ps, pr, es, er, ns,
 ):
     sec = lax.axis_index("section")
     shard = lax.axis_index("shard")
@@ -52,6 +52,13 @@
     peers.extend([((sec + d) % SECTIONS, shard) for d in range(1, SECTIONS)])
     for peer in peers:
         pl.semaphore_signal(barrier, inc=1, device_id=peer, device_id_type=MESH)
+
+    @pl.when(sec == 0)
+    def _():
+        for p in range(1, 2 * NZ):
+            _, place = dev((z + p // 2) % NZ, (xl + p) % 2, core)
+            pl.semaphore_signal(barrier, inc=1, device_id=(1, place), device_id_type=MESH)
+
     local = [
         pltpu.make_async_copy(source, target, ls.at[2 + n])
         for n, (source, target) in enumerate(
@@ -64,7 +71,21 @@
     ot_own[...] = o_raw[...].T
     own_v.wait()
     vt_own[...] = v_raw[...].T
-    pl.semaphore_wait(barrier, len(peers))
+
+    @pl.when(sec == 1)
+    def _():
+        pl.semaphore_wait(barrier, len(peers) + 2 * NZ - 1)
+
+    @pl.when(sec != 1)
+    def _():
+        pl.semaphore_wait(barrier, len(peers))
+
+    def ahead(n):
+        return pltpu.make_async_remote_copy(
+            src_ref=(gproj, vlow)[n], dst_ref=(gproj_in, vlow_in)[n], send_sem=es.at[n], recv_sem=er.at[n],
+            device_id=(up, shard), device_id_type=MESH,
+        )
+
 
     def v_block(z_, x_, c_, half):
         first = pl.multiple_of((z_ * 4 + x_ * 2 + c_) * cols, cols)
@@ -354,6 +375,11 @@
     local[2].wait()
     local[3].wait()
 
+    @pl.when(sec == 0)
+    def _():
+        ahead(0).start()
+
+
     def lowered(b, carry):
         rows = pl.ds(pl.multiple_of(b * ROWS, ROWS), ROWS)
         store_low[rows, :] = store[rows, :].astype(jnp.bfloat16)
@@ -396,25 +422,24 @@
 
     half_rows = gproj.shape[0] // 2
 
-    def features():
+    def features(source, right, values, own_feat):
         low = lax.dot_general(
-            c_in[...].reshape(LEN, width), gproj[...], (((1,), (1,)), ((), ())), preferred_element_type=jnp.float32
+            source[...].reshape(LEN, width), right[...], (((1,), (1,)), ((), ())), preferred_element_type=jnp.float32
         )
         feat[...] = lax.dot_general(
-            low, vlow[...], (((0,), (0,)), ((), ())),
+            low, values[...], (((0,), (0,)), ((), ())),
             precision=lax.Precision.HIGHEST, preferred_element_type=jnp.float32,
         )
         even = feat[pl.ds(0, half_rows, stride=2), :]
         odd = feat[pl.ds(1, half_rows, stride=2), :]
         packed = jnp.concatenate([even, odd], axis=1).astype(jnp.bfloat16)
-        feat_own[...] = packed
-        feats[shard] = packed
+        own_feat[...] = packed
 
     @pl.when(sec < SECTIONS - 1)
     def _():
         value_path()
 
-    def stage(b, top_layer, eager):
+    def stage(b, top_layer, eager, sending):
         rows = pl.ds(pl.multiple_of(b * ROWS, ROWS), ROWS)
         if eager:
             grad_value = jnp.zeros((ROWS, kv), jnp.float32)
@@ -437,15 +462,16 @@
             hidden = act[rows, span].astype(jnp.float32)
             grad_input = inverse * part - hidden * back
             c_out[b, :, span] = (c_in[b, :, span].astype(jnp.float32) + grad_input).astype(jnp.bfloat16)
-            c_copy(b, n).start()
-
-    def stages(top_layer):
+            if sending:
+                c_copy(b, n).start()
+
+    def stages(top_layer, sending):
         def one(b, carry):
-            stage(b, top_layer, False)
+            stage(b, top_layer, False, sending)
             return carry
 
         if not top_layer:
-            stage(0, False, True)
+            stage(0, False, True, sending)
         lax.fori_loop(0 if top_layer else 1, BLOCKS, one, 0)
 
     def rows_of(count):
@@ -475,26 +501,42 @@
 
     @pl.when(sec == 0)
     def _():
-        def one(b, carry):
-            for group in range(len(GROUPS)):
-                arrived(b, group)
-            return carry
-
-        lax.fori_loop(0, BLOCKS, one, 0)
-
-    @pl.when((sec > 0) & (sec < SECTIONS - 1))
-    def _():
-        stages(False)
+        ahead(1).start()
+
+    @pl.when((sec > 1) & (sec < SECTIONS - 1))
+    def _():
+        stages(False, True)
 
     @pl.when(sec == SECTIONS - 1)
     def _():
-        stages(True)
+        stages(True, True)
+
+    def n_copy(p):
+        return pltpu.make_async_remote_copy(
+            src_ref=feat_in, dst_ref=feats.at[shard], send_sem=ns.at[0], recv_sem=fr.at[p],
+            device_id=(down, dev((z + p // 2) % NZ, (xl + p) % 2, core)[1]), device_id_type=MESH,
+        )
+
+    near = (0, 1, 7, 2, 6, 3, 5, 4)
+    order = [2 * dz + dx for dz in near for dx in (0, 1)]
+
+    @pl.when(sec == 1)
+    def _():
+        stages(False, False)
+        ahead(0).wait_recv()
+        ahead(1).wait_recv()
+        features(c_out, gproj_in, vlow_in, feat_in)
+        for p in reversed(order):
+            n_copy(p).start()
 
     @pl.when(sec == SECTIONS - 1)
     def _():
         value_path()
 
-    features()
+    @pl.when(sec > 0)
+    def _():
+        features(c_in, gproj, vlow, feat_own)
+        feats[shard] = feat_own[...]
 
     def slot(p, c_):
         return ((z + NZ - p // 2) % NZ) * 4 + ((xl + p) % 2) * 2 + c_
@@ -515,7 +557,7 @@
     def g_copy(p):
         ref = feats.at[slot(p, core)]
         return pltpu.make_async_remote_copy(
-            src_ref=feat_own if p == 0 else ref, dst_ref=ref, send_sem=gs.at[0], recv_sem=gr.at[0],
+            src_ref=ref, dst_ref=ref, send_sem=gs.at[0], recv_sem=gr.at[0],
             device_id=dev(z, xl, 1 - core), device_id_type=MESH,
         )
 
@@ -526,14 +568,21 @@
             device_id=dev(z, xl, 1 - core), device_id_type=MESH,
         )
 
-    near = (0, 1, 7, 2, 6, 3, 5, 4)
-    order = [2 * dz + dx for dz in near for dx in (0, 1)][1:]
-    for p in reversed(order):
-        f_copy(p).start()
-    g_copy(0).start()
-    for p in order:
-        f_arrival(p).wait_recv()
-        g_copy(p).start()
+    @pl.when(sec > 0)
+    def _():
+        for p in reversed(order[1:]):
+            f_copy(p).start()
+        g_copy(0).start()
+        for p in order[1:]:
+            f_arrival(p).wait_recv()
+            g_copy(p).start()
+
+    @pl.when(sec == 0)
+    def _():
+        for p in order:
+            f_arrival(p).wait_recv()
+            g_copy(p).start()
+
     g_arrivals().wait_recv()
     gens = feats.shape[0]
     for q in range(gens):
@@ -562,10 +611,22 @@
 
     for d in range(1, SECTIONS):
         p_copy(d).start()
-    all_sent(fs, feats.at[pl.ds(0, 2 * NZ - 1)])
     all_sent(gs, feats.at[pl.ds(0, 2 * NZ)])
 
+    @pl.when(sec == 0)
+    def _():
+        ahead(0).wait_send()
+        ahead(1).wait_send()
+
+    @pl.when(sec == 1)
+    def _():
+        all_sent(ns, feats.at[pl.ds(0, 2 * NZ)])
+
     @pl.when(sec > 0)
+    def _():
+        all_sent(fs, feats.at[pl.ds(0, 2 * NZ - 1)])
+
+    @pl.when(sec > 1)
     def _():
         all_sent(cs, c_out)
 
@@ -617,6 +678,9 @@
             pltpu.VMEM((tokens, proj), f32),
             pltpu.VMEM((proj, proj), f32),
             pltpu.VMEM((proj // 2, 2 * proj), bf16),
+            pltpu.VMEM(gproj.shape, bf16),
+            pltpu.VMEM((tokens, proj), f32),
+            pltpu.VMEM((proj // 2, 2 * proj), bf16),
             pltpu.VMEM((gens, proj // 2, 2 * proj), bf16),
             pltpu.VMEM((gens * proj // 2, 2 * proj), f32),
             pltpu.VMEM((gens, proj * proj), bf16),
@@ -625,7 +689,7 @@
             dma((7,)),
             dma((1,)), dma((2, 4, 5)), dma((1,)), dma((10,)), dma((1,)), dma((6,)), dma((1,)), dma((9,)),
             dma((1,)), dma((BLOCKS, len(GROUPS))),
-            dma((1,)), dma((2 * NZ,)), dma((1,)), dma((1,)), dma((1,)), dma((1,)),
+            dma((1,)), dma((2 * NZ,)), dma((1,)), dma((1,)), dma((1,)), dma((1,)), dma((2,)), dma((2,)), dma((1,)),
         ],
         compiler_params=pltpu.CompilerParams(
             collective_id=0, has_side_effects=True, vmem_limit_bytes=60 * 1024 * 1024

time: 135 us -> 134 us (level)
  Pallas kernels: 134 us -> 132 us
    pallas_call x1, Pallas kernels: 134 us -> 132 us  [chain(): pl.pallas_call(chain_kernel, out_shape=jax.ShapeDtypeStruct((SECTIONS, ge...]
where the time goes in v5:
time: 134 us
  Pallas kernels  132 us (99%)
    pallas_call x1, Pallas kernels, chain(): pl.pallas_call(chain_kernel, out_shape=jax.ShapeDtypeStruct((SECTIONS, ge...  132 us

profile of v5, /device:TPU:7, one launch (start us, length us, event | category | flops | bytes accessed | tf_op | source)
XLA Modules:
  0.0 133.7 jit_solution(8422668588559750358)
XLA Ops:
  0.0 132.3 %shard_map.91 = f32[8,4,128]{2,1,0:T(4,128)} custom-call(bf16[96,4096]{1,0:T(8,128)(2,1)} %bitcast.12, bf16[96,4096]{1,0:T(8,128)(2,1)} %top_hbm.1, s32[1,96]{1,0:T(1,128)} %bitcast.17, f32[1,4096]{1,0:T(1,128)} %gain.1, bf16[128,1024]{1,0:T(8,128)(2,1)} %bitcast.14, bf16[1024,128]{1,0:T(8,128)(2,1)} %bitcast.15, bf16[64,1024]{1,0:T(8,128)(2,1)} %bitcast.16, ...), custom_call_target="tpu_custom_call" | custom-call | flops 3000000000 | bytes 4000000 | tf_op jit(solution)/shard_map/pallas_call | solution.py:653
  132.3 1.3 reduce_sum.9

commit v6 on v5

--- a/solution.py
+++ b/solution.py
@@ -13,7 +13,7 @@
 ROWS = 16
 BLOCKS = LEN // ROWS
 PIECES = 4
-GROUPS = ((0, 3), (3, 4))
+GROUPS = ((0, 2), (2, 3), (3, 4))
 
 
 def chain_kernel(

time: 134 us -> 134 us (level)
  no operation moved by 1% of the time
where the time goes in v6:
time: 134 us
  Pallas kernels  133 us (99%)
    pallas_call x1, Pallas kernels, chain(): pl.pallas_call(chain_kernel, out_shape=jax.ShapeDtypeStruct((SECTIONS, ge...  133 us

profile of v6, /device:TPU:7, one launch (start us, length us, event | category | flops | bytes accessed | tf_op | source)
XLA Modules:
  0.0 133.9 jit_solution(14090687477236061437)
XLA Ops:
  0.0 132.5 %shard_map.91 = f32[8,4,128]{2,1,0:T(4,128)} custom-call(bf16[96,4096]{1,0:T(8,128)(2,1)} %bitcast.12, bf16[96,4096]{1,0:T(8,128)(2,1)} %top_hbm.1, s32[1,96]{1,0:T(1,128)} %bitcast.17, f32[1,4096]{1,0:T(1,128)} %gain.1, bf16[128,1024]{1,0:T(8,128)(2,1)} %bitcast.14, bf16[1024,128]{1,0:T(8,128)(2,1)} %bitcast.15, bf16[64,1024]{1,0:T(8,128)(2,1)} %bitcast.16, ...), custom_call_target="tpu_custom_call" | custom-call | flops 3000000000 | bytes 4000000 | tf_op jit(solution)/shard_map/pallas_call | solution.py:653
  132.5 1.3 reduce_sum.9
